TPU v7x, 512 devices: a whole 4x8x8 slice. The times are simulated.
512 devices in a mesh: row: 16 (over z, core), col: 32 (over y, x).
Axes of the slice: x: 4, y: 8, z: 8, core: 2. Of those that a mesh axis runs over, the one named last changes fastest.
Arguments:
- data: bfloat16 [32768, 32768], P('row', 'col'), may hold values from 0 to 30
- w_rows: bfloat16 [64, 32768], P(None, 'row'), may hold values from 0 to 1
- h_init: float32 [64, 32768], P(None, 'col'), may hold values from 0 to 0.4
Outputs:
- h_scaled: bfloat16 [64, 32768], P(None, 'col')
- h_gram: float32 [64, 64], replicated
- w_terms: float32 [64, 32768], P(None, ('row', 'col'))
All inputs are finite; a program needn't handle non-finite values.
Results may differ from a plain program's by a relative error of at most 0.0005.
Values may be sent and summed in bfloat16 or wider, within the bound.
No kernel may reach another device: no remote copies, remote signals or barrier semaphores. Data moves between devices by JAX's collectives and lax.ppermute only.
A program may use at most 64 MiB of HBM per device.

v0:
```python
import math

import jax
import jax.numpy as jnp
from jax import lax
from jax.sharding import PartitionSpec as P

ITERS = 4


def in_blocks(x, dim, length):
    lengths = x.shape
    parts = x.reshape(*lengths[:dim], length, lengths[dim] // length, *lengths[dim + 1 :])
    return jnp.moveaxis(parts, dim, 0)


def summed_on_arrival(x, axis, dim):
    length = lax.axis_size(axis)
    parts = lax.all_to_all(in_blocks(x, dim, length), axis, 0, 0, tiled=True)
    return jnp.sum(parts, axis=0)


def rows_for(lines, length):
    spare = -lines.shape[0] % length
    if not spare:
        return lines
    return jnp.concatenate([lines, jnp.zeros((spare, *lines.shape[1:]), lines.dtype)])


def sent_to_all(x, axis):
    copies = jnp.broadcast_to(x, (lax.axis_size(axis), *x.shape))
    return lax.all_to_all(copies, axis, split_axis=0, concat_axis=0, tiled=True)


def in_order(parts, dim):
    parts = jnp.moveaxis(parts, 0, dim)
    lengths = parts.shape
    return parts.reshape(*lengths[:dim], lengths[dim] * lengths[dim + 1], *lengths[dim + 2 :])


def gathered_copies(x, axis, dim):
    parts = sent_to_all(x, axis)
    return in_order(parts, dim)


def nested_sum(x, axes):
    own = summed_on_arrival(rows_for(x, lax.axis_size(axes)), axes, 0)
    whole = gathered_copies(own, axes, 0)
    return whole[: len(x)].reshape(x.shape)


def in_one(arrays, axis):
    ends = [0]
    for a in arrays:
        ends.append(ends[-1] + a.size)
    subtotal = nested_sum(jnp.concatenate([a.ravel() for a in arrays]), axis)
    return tuple((subtotal[b:e].reshape(a.shape) for a, b, e in zip(arrays, ends, ends[1:])))


def over_copies(x, axis):
    everything = sent_to_all(x, axis)
    return jnp.sum(everything, axis=0)


def iterate(gram, target, start):
    lip = jnp.max(jnp.sum(gram, axis=1))
    factor = start
    ahead = start
    momentum = 1.0
    for step in range(ITERS):
        slope = jnp.dot(gram, ahead, precision=lax.Precision.HIGHEST) - target
        fresh = jnp.maximum(ahead - slope / lip, 0.0)
        following = (1.0 + math.sqrt(1.0 + 4.0 * momentum * momentum)) / 2.0
        ahead = fresh + (momentum - 1.0) / following * (fresh - factor)
        factor = fresh
        momentum = following
    return factor


def shards(data, w_rows, h_init):
    columns = h_init.shape[1] * lax.axis_size("col")
    local_target = jnp.dot(w_rows, data, preferred_element_type=jnp.float32)
    local_gram = lax.dot_general(
        w_rows, w_rows, (((1,), (1,)), ((), ())), preferred_element_type=jnp.float32
    )
    gram, target = in_one((local_gram, local_target), "row")
    factor = iterate(gram, target, h_init)
    squares = over_copies(jnp.sum(factor * factor, axis=1), "col")
    scale = lax.rsqrt(squares / columns + 1e-06)
    h_scaled = (factor * scale[:, None]).astype(jnp.bfloat16)
    local_outer = lax.dot_general(
        h_scaled, h_scaled, (((1,), (1,)), ((), ())), preferred_element_type=jnp.float32
    )
    h_gram = over_copies(local_outer, "col") / columns
    local_terms = lax.dot_general(
        h_scaled, data, (((1,), (1,)), ((), ())), preferred_element_type=jnp.float32
    )
    w_terms = summed_on_arrival(local_terms, "col", 1) / columns
    return (h_scaled, h_gram, w_terms)


def solution(mesh):
    in_specs = (P("row", "col"), P(None, "row"), P(None, "col"))
    out_specs = (P(None, "col"), P(), P(None, ("row", "col")))
    return jax.shard_map(shards, mesh=mesh, in_specs=in_specs, out_specs=out_specs, check_vma=False)
```

profile of v0, /device:TPU:1, one launch (start us, length us, event | category | flops | bytes accessed | tf_op | source)
XLA Modules:
  0.0 117.5 jit_solution(3484959014791852880)
XLA Ops:
  0.6 0.0 copy-start
  0.6 0.9 copy-done
  1.6 0.2 fusion.31
  1.8 0.0 copy-start.2
  1.8 3.1 %convolution_bitcast_fusion = f32[8,8,8,128]{3,2,1,0:T(8,128)S(1)} fusion(bf16[64,2048]{1,0:T(8,128)(2,1)S(1)} %copy-done, bf16[2048,1024]{1,0:T(8,128)(2,1)} %param.3), kind=kOutput, calls=%fused_computation.16 | convolution fusion | flops 268435456 | bytes 4718592 | tf_op jit(solution)/shard_map/dot_general | solution.py:82
  5.0 0.1 reshape.40
  5.0 23.6 %all_to_all.31 = f32[16,1,4352]{2,1,0:T(1,128)S(1)} all-to-all(f32[16,1,4352]{2,1,0:T(1,128)S(1)} %bitcast.18), channel_id=1, replica_groups=mesh['row'=16,'col'=32] {'row'}, dimensions={0} | all-to-all | bytes 557056 | tf_op jit(solution)/shard_map/all_to_all | solution.py:19
  28.6 0.2 reduce_sum.54
  28.8 0.1 broadcast_in_dim.10
  28.9 14.7 %all_to_all.32 = f32[16,1,4352]{2,1,0:T(1,128)S(1)} all-to-all(f32[16,1,4352]{2,1,0:T(1,128)S(1)} %broadcast_in_dim.10), channel_id=1, replica_groups=mesh['row'=16,'col'=32] {'row'}, dimensions={0} | all-to-all | bytes 557056 | tf_op jit(solution)/shard_map/all_to_all | solution.py:32
  43.7 0.7 reduce.2
  44.3 0.1 slice.12
  44.5 0.1 slice.14
  44.5 0.1 slice_reduce_fusion
  44.7 0.6 reduce_max.9
  45.3 0.0 copy-done.2
  45.3 1.0 fusion.11
  46.3 1.0 fusion.8
  47.4 1.0 fusion.5
  48.4 1.2 multiply_reduce_fusion
  49.6 18.1 %all_to_all.33 = f32[32,1,64]{2,1,0:T(1,128)S(1)} all-to-all(f32[32,1,64]{2,1,0:T(1,128)S(1)} %broadcast_in_dim.11), channel_id=1, replica_groups=mesh['row'=16,'col'=32] {'col'}, dimensions={0} | all-to-all | bytes 16384 | tf_op jit(solution)/shard_map/all_to_all | solution.py:32
  67.7 0.1 multiply_convert_fusion
  67.8 0.0 copy-start.1
  67.8 3.6 %fusion.33 = f32[64,2048]{1,0:T(8,128)S(1)} fusion(bf16[64,1024]{1,0:T(8,128)(2,1)S(1)} %multiply_convert_fusion, bf16[2048,1024]{1,0:T(8,128)(2,1)} %param.3), kind=kOutput, calls=%fused_computation.46 | convolution fusion | flops 268435456 | bytes 4849664 | tf_op jit(solution)/shard_map/dot_general | solution.py:95
  71.4 0.4 reshape.42
  71.9 0.6 copy.14
  72.5 1.5 %reshape.47 = f32[32,1,4096]{2,1,0:T(1,128)} reshape(f32[32,64,64]{2,1,0:T(8,128)S(1)} %bitcast.17) | data formatting | bytes 1048576
  73.9 3.9 %all-to-all-start.4 = ((f32[32,1,4096]{2,1,0:T(1,128)}), f32[32,1,4096]{2,1,0:T(1,128)S(1)}, u32[]{:S(2)}, u32[]{:S(2)}) async-start(f32[32,1,4096]{2,1,0:T(1,128)} %reshape.47), calls=%async_computation.4 | async-start | bytes 1048576 | tf_op jit(solution)/shard_map/all_to_all | solution.py:19
  77.8 0.0 copy-done.1
  77.9 0.2 fusion.32
  78.0 0.1 broadcast_in_dim.12
  78.1 1.4 %reshape.45 = f32[32,1,4096]{2,1,0:T(1,128)} reshape(f32[32,64,64]{2,1,0:T(8,128)S(1)} %broadcast_in_dim.12) | data formatting | bytes 1048576
  79.6 14.1 %all-to-all-done.4 = f32[32,1,4096]{2,1,0:T(1,128)S(1)} async-done(((f32[32,1,4096]{2,1,0:T(1,128)}), f32[32,1,4096]{2,1,0:T(1,128)S(1)}, u32[]{:S(2)}, u32[]{:S(2)}) %all-to-all-start.4) | async-done | bytes 524320 | tf_op jit(solution)/shard_map/all_to_all | solution.py:19
  93.7 5.8 %all-to-all-start.3 = ((f32[32,1,4096]{2,1,0:T(1,128)}), f32[32,1,4096]{2,1,0:T(1,128)S(1)}, u32[]{:S(2)}, u32[]{:S(2)}) async-start(f32[32,1,4096]{2,1,0:T(1,128)} %reshape.45), calls=%async_computation.3 | async-start | bytes 1048576 | tf_op jit(solution)/shard_map/all_to_all | solution.py:32
  99.5 0.5 broadcast.36
  100.0 1.9 %reduce.5 = f32[32,4096]{1,0:T(8,128)S(1)} reduce(f32[32,1,4096]{2,1,0:T(1,128)S(1)} %all-to-all-done.4, f32[]{:T(128)} %broadcast.36), dimensions={1}, to_apply=%all_to_all.25.reduce_sub_computation | reduce | bytes 1048580 | tf_op jit(solution)/shard_map/all_to_all | solution.py:19
  101.9 0.4 reshape.48
  102.3 0.1 reduce_sum.59
  102.4 0.6 broadcast_multiply_fusion
  103.0 11.4 %all-to-all-done.3 = f32[32,1,4096]{2,1,0:T(1,128)S(1)} async-done(((f32[32,1,4096]{2,1,0:T(1,128)}), f32[32,1,4096]{2,1,0:T(1,128)S(1)}, u32[]{:S(2)}, u32[]{:S(2)}) %all-to-all-start.3) | async-done | bytes 524320 | tf_op jit(solution)/shard_map/all_to_all | solution.py:32
  114.5 1.9 %reduce.4 = f32[32,4096]{1,0:T(8,128)S(1)} reduce(f32[32,1,4096]{2,1,0:T(1,128)S(1)} %all-to-all-done.3, f32[]{:T(128)} %broadcast.36), dimensions={1}, to_apply=%all_to_all.24.reduce_sub_computation | reduce | bytes 1048580 | tf_op jit(solution)/shard_map/all_to_all | solution.py:32
  116.4 0.4 reshape.46
  116.8 0.1 reduce_sum.58
  116.9 0.6 broadcast_multiply_fusion.1
  (5 shorter events, 0.1 us)
Async XLA Ops:
  0.6 1.0 copy-start
  1.8 43.5 %copy-start.2 = (f32[64,1024]{1,0:T(8,128)S(1)}, f32[64,1024]{1,0:T(8,128)}, u32[]{:S(2)}) copy-start(f32[64,1024]{1,0:T(8,128)} %param.5) | copy-start | bytes 786436
  67.8 10.0 %copy-start.1 = (bf16[64,1024]{1,0:T(8,128)(2,1)}, bf16[64,1024]{1,0:T(8,128)(2,1)S(1)}, u32[]{:S(2)}) copy-start(bf16[64,1024]{1,0:T(8,128)(2,1)S(1)} %multiply_convert_fusion) | copy-start | bytes 393220
  73.9 19.8 %all-to-all-start.4 = ((f32[32,1,4096]{2,1,0:T(1,128)}), f32[32,1,4096]{2,1,0:T(1,128)S(1)}, u32[]{:S(2)}, u32[]{:S(2)}) async-start(f32[32,1,4096]{2,1,0:T(1,128)} %reshape.47), calls=%async_computation.4 | async-start | bytes 1048576 | tf_op jit(solution)/shard_map/all_to_all | solution.py:19
  93.7 20.7 %all-to-all-start.3 = ((f32[32,1,4096]{2,1,0:T(1,128)}), f32[32,1,4096]{2,1,0:T(1,128)S(1)}, u32[]{:S(2)}, u32[]{:S(2)}) async-start(f32[32,1,4096]{2,1,0:T(1,128)} %reshape.45), calls=%async_computation.3 | async-start | bytes 1048576 | tf_op jit(solution)/shard_map/all_to_all | solution.py:32
where the time goes:
time: 120 us; the launch traced here: 117 us
  blocking collectives  56.4 us (47%)
  waiting for transfers between devices  25.5 us (21%)
  matrix products  11.3 us (9%)
  starting transfers between devices  9.64 us (8%)
  other arithmetic  6.89 us (6%)
  local copies, waits for them, and re-layouts  6.84 us (6%)
    all_to_all x2, blocking collectives, sent_to_all(): return lax.all_to_all(copies, axis, split_axis=0, concat_axis=0, tiled=True)  32.8 us
    all_to_all x1, blocking collectives, summed_on_arrival(): parts = lax.all_to_all(in_blocks(x, dim, length), axis, 0, 0, tiled=True)  23.6 us
    all_to_all x1, waiting for transfers between devices, summed_on_arrival(): parts = lax.all_to_all(in_blocks(x, dim, length), axis, 0, 0, tiled=True)  14.1 us
    all_to_all x1, waiting for transfers between devices, sent_to_all(): return lax.all_to_all(copies, axis, split_axis=0, concat_axis=0, tiled=True)  11.4 us
    all_to_all x1, starting transfers between devices, sent_to_all(): return lax.all_to_all(copies, axis, split_axis=0, concat_axis=0, tiled=True)  5.75 us
    unnamed x11, local copies, waits for them, and re-layouts  4.74 us
    dot_general x4, matrix products, iterate(): slope = jnp.dot(gram, ahead, precision=lax.Precision.HIGHEST) - target  4.27 us
    all_to_all x1, starting transfers between devices, summed_on_arrival(): parts = lax.all_to_all(in_blocks(x, dim, length), axis, 0, 0, tiled=True)  3.89 us
  transfers between devices with their start and end apart: 2, of which 2 were waited for; matrix products, arithmetic and copies ran while one was open for 4% of the time, Pallas kernels for 0%

commit v1 on v0

v1 whole, which is shorter than its diff:
```python
import math

import jax
import jax.numpy as jnp
from jax import lax
from jax.experimental import pallas as pl
from jax.experimental.pallas import tpu as pltpu
from jax.sharding import PartitionSpec as P

ITERS = 4
LANES = 128
HALF = 64
MIB = 1 << 20


def low_lanes(x):
    return lax.broadcasted_iota(jnp.int32, x.shape, 1) < HALF


def turned(x):
    return pltpu.roll(x, HALF, 1)


def stack_sides(x):
    return jnp.where(low_lanes(x[:32]), x[:32], turned(x[32:]))


def stack_copies(x):
    return jnp.where(low_lanes(x[:32]), x[:32], x[32:])


def unstack(x):
    return jnp.concatenate([x, turned(x)], axis=0)


def halves_of_rank(spot_ref, w_ref, data_ref, h_ref, own_ref, send_ref, chunk_ref, acc, gacc):
    step = pl.program_id(0)

    @pl.when(step == 0)
    def _():
        acc[...] = jnp.zeros_like(acc)
        gacc[...] = jnp.zeros_like(gacc)
        start = h_ref[...]
        chunk_ref[...] = jnp.where(spot_ref[2] == 0, start, turned(start))

    w = w_ref[...]
    acc[...] += jnp.dot(w, data_ref[...], preferred_element_type=jnp.float32)
    gacc[...] += lax.dot_general(
        w, jnp.concatenate([w, w], axis=0), (((1,), (1,)), ((), ())), preferred_element_type=jnp.float32
    )

    @pl.when(step == pl.num_programs(0) - 1)
    def _():
        width = acc.shape[1] // 2
        first = spot_ref[0] == 0
        left = acc[:, :width]
        right = acc[:, width:]
        own_ref[:, :width] = jnp.where(first, left, right)
        send_ref[:, :width] = jnp.where(first, right, left)
        own_ref[:, width:] = gacc[...]
        send_ref[:, width:] = gacc[...]


def partial_products(spot, w_rows, data, h_init):
    rows, columns = data.shape
    rank = w_rows.shape[0]
    blocks = 4
    depth = rows // blocks
    out = jax.ShapeDtypeStruct((rank, columns // 2 + LANES), jnp.float32)
    whole = lambda i, spot: (0, 0)
    return pl.pallas_call(
        halves_of_rank,
        grid_spec=pltpu.PrefetchScalarGridSpec(
            num_scalar_prefetch=1,
            grid=(blocks,),
            in_specs=[
                pl.BlockSpec((rank, depth), lambda i, spot: (0, i)),
                pl.BlockSpec((depth, columns), lambda i, spot: (i, 0)),
                pl.BlockSpec((rank, LANES), lambda i, spot: (0, spot[1])),
            ],
            out_specs=[
                pl.BlockSpec(out.shape, whole),
                pl.BlockSpec(out.shape, whole),
                pl.BlockSpec((rank, LANES), whole),
            ],
            scratch_shapes=[pltpu.VMEM((rank, columns), jnp.float32), pltpu.VMEM((rank, LANES), jnp.float32)],
        ),
        out_shape=[out, out, jax.ShapeDtypeStruct((rank, LANES), jnp.float32)],
        compiler_params=pltpu.CompilerParams(vmem_limit_bytes=24 * MIB),
        name="products",
    )(spot, w_rows, data, h_init)


def packing(zs, own_ref, got_ref, out_ref):
    width = own_ref.shape[1] - LANES
    gram = stack_copies(own_ref[:, width:] + got_ref[:, width:])
    for tile in range(width // LANES):
        at = slice(tile * LANES, (tile + 1) * LANES)
        x = own_ref[:, at] + got_ref[:, at]
        top, low = x[:32], x[32:]
        left = low_lanes(top)
        for side, block in enumerate((jnp.where(left, top, turned(low)), jnp.where(left, turned(top), low))):
            base = (2 * tile + side) * 64
            out_ref[base : base + 32, :] = block
            out_ref[base + 32 : base + 64, :] = gram


def packed(zs, own, got):
    return pl.pallas_call(
        lambda *refs: packing(zs, *refs),
        out_shape=jax.ShapeDtypeStruct((zs * 64, LANES), jnp.float32),
        compiler_params=pltpu.CompilerParams(vmem_limit_bytes=8 * MIB),
        name="packing",
    )(own, got)


def iterating(zs, got_ref, start_ref, out_ref):
    total = got_ref[0:64, :]
    for part in range(1, zs):
        total = total + got_ref[part * 64 : part * 64 + 64, :]
    target = unstack(total[:32])
    gram = unstack(total[32:])[:, :HALF]
    lip = jnp.max(jnp.sum(gram, axis=1, keepdims=True))
    factor = start_ref[...]
    ahead = factor
    momentum = 1.0
    for step in range(ITERS):
        slope = jnp.dot(
            gram, ahead, precision=lax.Precision.HIGHEST, preferred_element_type=jnp.float32
        ) - target
        fresh = jnp.maximum(ahead - slope / lip, 0.0)
        following = (1.0 + math.sqrt(1.0 + 4.0 * momentum * momentum)) / 2.0
        ahead = fresh + (momentum - 1.0) / following * (fresh - factor)
        factor = fresh
        momentum = following
    block = stack_sides(factor)
    for part in range(zs):
        out_ref[part * 32 : part * 32 + 32, :] = block


def iterated(zs, got, start):
    return pl.pallas_call(
        lambda *refs: iterating(zs, *refs),
        out_shape=jax.ShapeDtypeStruct((zs * 32, LANES), jnp.float32),
        compiler_params=pltpu.CompilerParams(vmem_limit_bytes=8 * MIB),
        name="iterating",
    )(got, start)


def contracting(zs, spot_ref, own_ref, other_ref, data_ref, factor_ref, out_ref, lines, gram):
    step = pl.program_id(0)
    width = zs * HALF

    @pl.when(step == 0)
    def _():
        first = spot_ref[0] == 0
        for tile in range(zs // 2):
            a0, b0 = own_ref[tile * 64 : tile * 64 + 32, :], own_ref[tile * 64 + 32 : tile * 64 + 64, :]
            a1, b1 = other_ref[tile * 64 : tile * 64 + 32, :], other_ref[tile * 64 + 32 : tile * 64 + 64, :]
            for side in range(2):
                a = jnp.where(first, a0, a1) if side == 0 else jnp.where(first, a1, a0)
                b = jnp.where(first, b0, b1) if side == 0 else jnp.where(first, b1, b0)
                left = low_lanes(a)
                x = jnp.concatenate([jnp.where(left, a, turned(b)), jnp.where(left, turned(a), b)], axis=0)
                at = slice(side * width + tile * LANES, side * width + (tile + 1) * LANES)
                factor_ref[:, at] = x
                low = x.astype(jnp.bfloat16)
                lines[0:64, at] = low
                lines[64:128, at] = low
        factor = factor_ref[...]
        squares = jnp.sum(factor * factor, axis=1, keepdims=True)
        outer = lax.dot_general(
            lines[0:64, :], lines[...], (((1,), (1,)), ((), ())), preferred_element_type=jnp.float32
        )
        row = lax.broadcasted_iota(jnp.int32, outer.shape, 0)
        lane = lax.broadcasted_iota(jnp.int32, outer.shape, 1)
        gram[...] = stack_copies(jnp.where(row == lane % HALF, squares, outer))

    terms = lax.dot_general(
        data_ref[...], lines[...], (((1,), (1,)), ((), ())), preferred_element_type=jnp.float32
    )
    for part in range(terms.shape[0] // 64):
        out_ref[part * 64 : part * 64 + 32, :] = stack_copies(terms[part * 64 : part * 64 + 64])
        out_ref[part * 64 + 32 : part * 64 + 64, :] = gram[...]


def contracted(zs, spot, own, other, data):
    rows, columns = data.shape
    blocks = 4
    depth = rows // blocks
    whole = lambda i, spot: (0, 0)
    return pl.pallas_call(
        lambda *refs: contracting(zs, *refs),
        grid_spec=pltpu.PrefetchScalarGridSpec(
            num_scalar_prefetch=1,
            grid=(blocks,),
            in_specs=[
                pl.BlockSpec(own.shape, whole),
                pl.BlockSpec(own.shape, whole),
                pl.BlockSpec((depth, columns), lambda i, spot: (i, 0)),
            ],
            out_specs=[
                pl.BlockSpec((64, columns), whole),
                pl.BlockSpec((depth, LANES), lambda i, spot: (i, 0)),
            ],
            scratch_shapes=[pltpu.VMEM((LANES, columns), jnp.bfloat16), pltpu.VMEM((32, LANES), jnp.float32)],
        ),
        out_shape=[
            jax.ShapeDtypeStruct((64, columns), jnp.float32),
            jax.ShapeDtypeStruct((rows, LANES), jnp.float32),
        ],
        compiler_params=pltpu.CompilerParams(vmem_limit_bytes=24 * MIB),
        name="contracting",
    )(spot, own, other, data)


def finishing(count, columns, got_ref, factor_ref, scaled_ref, gram_ref, terms_ref):
    total = got_ref[0:64, :]
    for part in range(1, count):
        total = total + got_ref[part * 64 : part * 64 + 64, :]
    outer = unstack(total[32:])
    row = lax.broadcasted_iota(jnp.int32, outer.shape, 0)
    lane = lax.broadcasted_iota(jnp.int32, outer.shape, 1)
    diagonal = jnp.where(row == lane, outer, 0.0)

    def scale_of(squares):
        mean = squares / columns + 1e-06
        first = lax.rsqrt(mean)
        return first * (1.5 - 0.5 * mean * first * first)

    down = scale_of(jnp.sum(diagonal, axis=1, keepdims=True))
    across = scale_of(jnp.sum(diagonal, axis=0, keepdims=True))
    scaled_ref[...] = (factor_ref[...] * down).astype(jnp.bfloat16)
    gram_ref[...] = (outer * down * across / columns)[:, :HALF]
    terms = jnp.transpose(unstack(total[:32]))[:HALF, :]
    terms_ref[...] = terms * down / columns


def finished(count, columns, got, factor):
    return pl.pallas_call(
        lambda *refs: finishing(count, columns, *refs),
        out_shape=[
            jax.ShapeDtypeStruct(factor.shape, jnp.bfloat16),
            jax.ShapeDtypeStruct((64, 64), jnp.float32),
            jax.ShapeDtypeStruct((64, 64), jnp.float32),
        ],
        compiler_params=pltpu.CompilerParams(vmem_limit_bytes=8 * MIB),
        name="finishing",
    )(got, factor)


def shards(data, w_rows, h_init):
    rows = lax.axis_size("row")
    zs = rows // 2
    columns = data.shape[1] * lax.axis_size("col")
    me = lax.axis_index("row")
    core, level = me % 2, me // 2
    at = core * (data.shape[1] // 2) + level * HALF
    spot = jnp.stack([core, at // LANES, level % 2]).astype(jnp.int32)
    swap = [(2 * z + c, 2 * z + 1 - c) for z in range(zs) for c in range(2)]
    level_groups = [[2 * z + c for z in range(zs)] for c in range(2)]

    own, send, start = partial_products(spot, w_rows, data, h_init)
    got = lax.ppermute(send, "row", swap)
    parts = packed(zs, own, got)
    parts = lax.all_to_all(parts, "row", 0, 0, tiled=True, axis_index_groups=level_groups)
    copies = iterated(zs, parts, start)
    mine = lax.all_to_all(copies, "row", 0, 0, tiled=True, axis_index_groups=level_groups)
    other = lax.ppermute(mine, "row", swap)
    factor, terms = contracted(zs, spot, mine, other, data)
    sums = lax.all_to_all(terms, "col", 0, 0, tiled=True)
    return tuple(finished(lax.axis_size("col"), columns, sums, factor))


def solution(mesh):
    in_specs = (P("row", "col"), P(None, "row"), P(None, "col"))
    out_specs = (P(None, "col"), P(), P(None, ("row", "col")))
    return jax.shard_map(shards, mesh=mesh, in_specs=in_specs, out_specs=out_specs, check_vma=False)
```

time: 120 us -> 90.6 us (0.76)
  waiting for transfers between devices: 25.5 us -> 1.97 us
  matrix products: 11.3 us -> 0 us
  other arithmetic: 6.89 us -> 0.08 us
  Pallas kernels: 0 us -> 6.65 us
  blocking collectives: 56.4 us -> 61.8 us
  starting transfers between devices: 9.64 us -> 13.5 us
  local copies, waits for them, and re-layouts: 6.84 us -> 4.09 us
    all_to_all x2 -> x0, waiting for transfers between devices: 25.5 us -> none  [the longest x1 14.1 us: summed_on_arrival(): parts = lax.all_to_all(in_blocks(x, dim, length), axis, 0, 0, tiled=True)]
    ppermute x0 -> x2, starting transfers between devices: none -> 13.5 us  [the longest x1 8.75 us: shards(): got = lax.ppermute(send, 'row', swap)]
    dot_general x8 -> x0, matrix products: 11.3 us -> none  [the longest x4 4.27 us: iterate(): slope = jnp.dot(gram, ahead, precision=lax.Precision.HIGHEST) - target]
    all_to_all x2 -> x0, starting transfers between devices: 9.64 us -> none  [the longest x1 5.75 us: sent_to_all(): return lax.all_to_all(copies, axis, split_axis=0, concat_axis=0, tiled=True)]
    pallas_call x0 -> x5, Pallas kernels: none -> 6.65 us  [the longest x1 2.64 us: contracted(): pl.pallas_call(lambda *refs: contracting(zs, *refs), grid_spec=pltpu.Pref...]
    all_to_all x3, blocking collectives: 56.4 us -> 61.8 us  [the longest x1 35.9 us: shards(): sums = lax.all_to_all(terms, 'col', 0, 0, tiled=True)]
    all_to_all x3 -> x0, other arithmetic: 4.44 us -> none  [the longest x2 2.55 us: sent_to_all(): return lax.all_to_all(copies, axis, split_axis=0, concat_axis=0, tiled=True)]
    ppermute x0 -> x2, waiting for transfers between devices: none -> 1.97 us  [the longest x1 1.01 us: shards(): got = lax.ppermute(send, 'row', swap)]
  transfers between devices with their start and end apart: 2 -> 2, of which waited for: 2 -> 2; matrix products, arithmetic and copies ran while one was open for 4% -> 0% of each run, Pallas kernels for 0% -> 0%
where the time goes in v1:
time: 90.6 us; the launch traced here: 88.8 us
  blocking collectives  61.8 us (68%)
  starting transfers between devices  13.5 us (15%)
  Pallas kernels  6.65 us (7%)
  local copies, waits for them, and re-layouts  4.09 us (5%)
  waiting for transfers between devices  1.97 us (2%)
    all_to_all x1, blocking collectives, shards(): sums = lax.all_to_all(terms, 'col', 0, 0, tiled=True)  35.9 us
    all_to_all x1, blocking collectives, shards(): lax.all_to_all(parts, 'row', 0, 0, tiled=True, axis_index_groups=level_gr...  15.6 us
    all_to_all x1, blocking collectives, shards(): lax.all_to_all(copies, 'row', 0, 0, tiled=True, axis_index_groups=level_g...  10.3 us
    ppermute x1, starting transfers between devices, shards(): got = lax.ppermute(send, 'row', swap)  8.75 us
    ppermute x1, starting transfers between devices, shards(): other = lax.ppermute(mine, 'row', swap)  4.72 us
    unnamed x8, local copies, waits for them, and re-layouts  4.09 us
    pallas_call x1, Pallas kernels, contracted(): pl.pallas_call(lambda *refs: contracting(zs, *refs), grid_spec=pltpu.Pref...  2.64 us
    pallas_call x1, Pallas kernels, partial_products(): pl.pallas_call(halves_of_rank, grid_spec=pltpu.PrefetchScalarGridSpec(num...  2.19 us
  transfers between devices with their start and end apart: 2, of which 2 were waited for; matrix products, arithmetic and copies ran while one was open for 0% of the time, Pallas kernels for 0%

profile of v1, /device:TPU:1, one launch (start us, length us, event | category | flops | bytes accessed | tf_op | source)
XLA Modules:
  0.0 88.8 jit_solution(12283629984349473741)
XLA Ops:
  0.7 0.1 pad_add_fusion.spot_ref.refs_0_
  0.8 0.0 copy-start
  0.8 2.2 %copy-done = bf16[2048,1024]{1,0:T(8,128)(2,1)S(1)} copy-done((bf16[2048,1024]{1,0:T(8,128)(2,1)S(1)}, bf16[2048,1024]{1,0:T(8,128)(2,1)}, u32[]{:S(2)}) %copy-start) | copy-done | bytes 4194328
  3.0 0.0 copy-start.2
  3.0 0.9 %copy-done.2 = bf16[64,2048]{1,0:T(8,128)(2,1)S(1)} copy-done((bf16[64,2048]{1,0:T(8,128)(2,1)S(1)}, bf16[64,2048]{1,0:T(8,128)(2,1)}, u32[]{:S(2)}) %copy-start.2) | copy-done | bytes 262168
  3.9 0.0 copy-start.3
  3.9 0.9 %copy-done.3 = f32[64,1024]{1,0:T(8,128)S(1)} copy-done((f32[64,1024]{1,0:T(8,128)S(1)}, f32[64,1024]{1,0:T(8,128)}, u32[]{:S(2)}) %copy-start.3) | copy-done | bytes 262168
  4.9 0.0 copy-start.1
  4.9 2.2 %products.1 = (f32[64,640]{1,0:T(8,128)S(1)}, f32[64,640]{1,0:T(8,128)S(1)}, f32[64,128]{1,0:T(8,128)S(1)}) custom-call(s32[3]{0:T(128)S(1)} %pad_add_fusion.spot_ref.refs_0_, bf16[64,2048]{1,0:T(8,128)(2,1)S(1)} %copy-done.2, bf16[2048,1024]{1,0:T(8,128)(2,1)S(1)} %copy-done, f32[64,1024]{1,0:T(8,128)S(1)} %copy-done.3), custom_call_target="tpu_custom_call" | custom-call | tf_op jit(solution)/shard_map/products/pallas_call | solution.py:71
  7.1 8.7 %collective-permute-start = (f32[64,640]{1,0:T(8,128)S(1)}, f32[64,640]{1,0:T(8,128)S(1)}, u32[]{:S(2)}, u32[]{:S(2)}) collective-permute-start(f32[64,640]{1,0:T(8,128)S(1)} %get-tuple-element.9), channel_id=1, source_target_pairs={{0,32},{32,0},{64,96},{96,64},{128,160},{160,128},{192,224},{224,1... | collective-permute-start | bytes 491528 | tf_op jit(solution)/shard_map/ppermute | solution.py:264
  15.8 1.0 %collective-permute-done.refs_1_ = f32[64,640]{1,0:T(8,128)S(1)} collective-permute-done((f32[64,640]{1,0:T(8,128)S(1)}, f32[64,640]{1,0:T(8,128)S(1)}, u32[]{:S(2)}, u32[]{:S(2)}) %collective-permute-start) | collective-permute-done | bytes 163872 | tf_op jit(solution)/shard_map/ppermute | solution.py:264
  16.8 0.1 packing.1
  16.9 15.6 %all_to_all.33 = f32[8,64,128]{2,1,0:T(8,128)S(1)} all-to-all(f32[8,64,128]{2,1,0:T(8,128)S(1)} %bitcast.11), channel_id=1, replica_groups={{0,64,128,192,256,320,384,448},{32,96,160,224,288,352,416,480},{1,65,12..., dimensions={0} | all-to-all | bytes 524288 | tf_op jit(solution)/shard_map/all_to_all | solution.py:266
  32.6 0.8 iterating.1
  33.4 10.3 %all_to_all.34 = f32[8,32,128]{2,1,0:T(8,128)S(1)} all-to-all(f32[8,32,128]{2,1,0:T(8,128)S(1)} %bitcast.15), channel_id=1, replica_groups={{0,64,128,192,256,320,384,448},{32,96,160,224,288,352,416,480},{1,65,12..., dimensions={0} | all-to-all | bytes 262144 | tf_op jit(solution)/shard_map/all_to_all | solution.py:268
  43.7 4.7 %collective-permute-start.1 = (f32[256,128]{1,0:T(8,128)S(1)}, f32[256,128]{1,0:T(8,128)S(1)}, u32[]{:S(2)}, u32[]{:S(2)}) collective-permute-start(f32[256,128]{1,0:T(8,128)S(1)} %bitcast.13), channel_id=1, source_target_pairs={{0,32},{32,0},{64,96},{96,64},{128,160},{160,128},{192,224},{224,1... | collective-permute-start | bytes 393224 | tf_op jit(solution)/shard_map/ppermute | solution.py:269
  48.5 1.0 %collective-permute-done.1.refs_2_ = f32[256,128]{1,0:T(8,128)S(1)} collective-permute-done((f32[256,128]{1,0:T(8,128)S(1)}, f32[256,128]{1,0:T(8,128)S(1)}, u32[]{:S(2)}, u32[]{:S(2)}) %collective-permute-start.1) | collective-permute-done | bytes 131104 | tf_op jit(solution)/shard_map/ppermute | solution.py:269
  49.4 0.0 copy-done.1
  49.4 2.6 %contracting.1 = (f32[64,1024]{1,0:T(8,128)S(1)}, f32[2048,128]{1,0:T(8,128)S(1)}) custom-call(s32[3]{0:T(128)S(1)} %pad_add_fusion.spot_ref.refs_0_, f32[256,128]{1,0:T(8,128)S(1)} %bitcast.14, f32[256,128]{1,0:T(8,128)S(1)} %collective-permute-done.1.refs_2_, bf16[2048,1024]{1,0:T(8,128)(2,1)S(1)} %copy-done.1), custom_call_target="tpu_custom_call" | custom-call | tf_op jit(solution)/shard_map/contracting/pallas_call | solution.py:192
  52.1 35.9 %all_to_all.35 = f32[32,64,128]{2,1,0:T(8,128)S(1)} all-to-all(f32[32,64,128]{2,1,0:T(8,128)S(1)} %bitcast.10), channel_id=1, replica_groups=mesh['row'=16,'col'=32] {'col'}, dimensions={0} | all-to-all | bytes 2097152 | tf_op jit(solution)/shard_map/all_to_all | solution.py:271
  87.9 0.9 finishing.1
Async XLA Ops:
  0.8 2.2 %copy-start = (bf16[2048,1024]{1,0:T(8,128)(2,1)S(1)}, bf16[2048,1024]{1,0:T(8,128)(2,1)}, u32[]{:S(2)}) copy-start(bf16[2048,1024]{1,0:T(8,128)(2,1)} %refs_3_.1) | copy-start | bytes 12582916
  3.0 0.9 %copy-start.2 = (bf16[64,2048]{1,0:T(8,128)(2,1)S(1)}, bf16[64,2048]{1,0:T(8,128)(2,1)}, u32[]{:S(2)}) copy-start(bf16[64,2048]{1,0:T(8,128)(2,1)} %w_ref.1) | copy-start | bytes 786436
  3.9 0.9 %copy-start.3 = (f32[64,1024]{1,0:T(8,128)S(1)}, f32[64,1024]{1,0:T(8,128)}, u32[]{:S(2)}) copy-start(f32[64,1024]{1,0:T(8,128)} %h_ref.1) | copy-start | bytes 786436
  4.9 44.6 %copy-start.1 = (bf16[2048,1024]{1,0:T(8,128)(2,1)S(1)}, bf16[2048,1024]{1,0:T(8,128)(2,1)}, u32[]{:S(2)}) copy-start(bf16[2048,1024]{1,0:T(8,128)(2,1)} %refs_3_.1) | copy-start | bytes 12582916
  7.1 9.8 %collective-permute-start = (f32[64,640]{1,0:T(8,128)S(1)}, f32[64,640]{1,0:T(8,128)S(1)}, u32[]{:S(2)}, u32[]{:S(2)}) collective-permute-start(f32[64,640]{1,0:T(8,128)S(1)} %get-tuple-element.9), channel_id=1, source_target_pairs={{0,32},{32,0},{64,96},{96,64},{128,160},{160,128},{192,224},{224,1... | collective-permute-start | bytes 491528 | tf_op jit(solution)/shard_map/ppermute | solution.py:264
  43.7 5.7 %collective-permute-start.1 = (f32[256,128]{1,0:T(8,128)S(1)}, f32[256,128]{1,0:T(8,128)S(1)}, u32[]{:S(2)}, u32[]{:S(2)}) collective-permute-start(f32[256,128]{1,0:T(8,128)S(1)} %bitcast.13), channel_id=1, source_target_pairs={{0,32},{32,0},{64,96},{96,64},{128,160},{160,128},{192,224},{224,1... | collective-permute-start | bytes 393224 | tf_op jit(solution)/shard_map/ppermute | solution.py:269

commit v2 on v1

v2 whole, which is shorter than its diff:
```python
import math

import jax
import jax.numpy as jnp
from jax import lax
from jax.experimental import pallas as pl
from jax.experimental.pallas import tpu as pltpu
from jax.sharding import PartitionSpec as P

ITERS = 4
LOG2E = 1.4426950408889634
LANES = 128
HALF = 64
BLOCKS = 4
CHUNK = 56
MIB = 1 << 20


def low_lanes(x):
    return lax.broadcasted_iota(jnp.int32, x.shape, 1) < HALF


def turned(x):
    return pltpu.roll(x, HALF, 1)


def stack_sides(x):
    return jnp.where(low_lanes(x[:32]), x[:32], turned(x[32:]))


def stack_copies(x):
    return jnp.where(low_lanes(x[:32]), x[:32], x[32:])


def unstack(x):
    return jnp.concatenate([x, turned(x)], axis=0)


def multiplying(zs, w_hbm, data_hbm, h_hbm, own_ref, send_ref, start_ref, data_ref, w, h, acc, sems):
    rows, columns = data_ref.shape
    width = columns // 2
    depth = rows // BLOCKS
    me = lax.axis_index("row")
    core, level = lax.rem(me, 2), lax.div(me, 2)
    tile = core * (width // LANES) + lax.div(level, 2)
    copies = [
        pltpu.make_async_copy(w_hbm, w, sems.at[BLOCKS]),
        pltpu.make_async_copy(
            h_hbm.at[:, pl.ds(pl.multiple_of(tile * LANES, LANES), LANES)], h, sems.at[BLOCKS + 1]
        ),
    ]
    for block in range(BLOCKS):
        at = pl.ds(block * depth, depth)
        copies.append(pltpu.make_async_copy(data_hbm.at[at, :], data_ref.at[at, :], sems.at[block]))
    for copy in (copies[0], *copies[2:], copies[1]):
        copy.start()
    copies[0].wait()
    gram = lax.dot_general(
        w[...], jnp.concatenate([w[...], w[...]], axis=0), (((1,), (1,)), ((), ())), preferred_element_type=jnp.float32
    )
    own_ref[:, width:] = gram
    send_ref[:, width:] = gram
    for block in range(BLOCKS):
        copies[2 + block].wait()
        at = slice(block * depth, (block + 1) * depth)
        part = jnp.dot(w[:, at], data_ref[at, :], preferred_element_type=jnp.float32)
        if block == 0:
            acc[...] = part
        else:
            acc[...] += part
    first = core == 0
    left = acc[:, :width]
    right = acc[:, width:]
    own_ref[:, :width] = jnp.where(first, left, right)
    send_ref[:, :width] = jnp.where(first, right, left)
    copies[1].wait()
    begin = h[...]
    start_ref[...] = jnp.where(lax.rem(level, 2) == 0, begin, turned(begin))


def multiplied(zs, w_rows, data, h_init):
    rows, columns = data.shape
    rank = w_rows.shape[0]
    half = jax.ShapeDtypeStruct((rank, columns // 2 + LANES), jnp.float32)
    start = jax.ShapeDtypeStruct((rank, LANES), jnp.float32)
    return pl.pallas_call(
        lambda *refs: multiplying(zs, *refs),
        in_specs=[pl.BlockSpec(memory_space=pl.ANY)] * 3,
        out_specs=[pl.BlockSpec(memory_space=pltpu.VMEM)] * 3,
        out_shape=[half, half, start],
        scratch_shapes=[
            pltpu.VMEM(data.shape, data.dtype),
            pltpu.VMEM(w_rows.shape, w_rows.dtype),
            pltpu.VMEM((rank, LANES), jnp.float32),
            pltpu.VMEM((rank, columns), jnp.float32),
            pltpu.SemaphoreType.DMA((BLOCKS + 2,)),
        ],
        compiler_params=pltpu.CompilerParams(vmem_limit_bytes=56045568),
        name="multiplying",
    )(w_rows, data, h_init)


def packing(zs, own_ref, got_ref, out_ref):
    width = own_ref.shape[1] - LANES
    gram = stack_copies(own_ref[:, width:] + got_ref[:, width:])
    for tile in range(width // LANES):
        at = slice(tile * LANES, (tile + 1) * LANES)
        x = own_ref[:, at] + got_ref[:, at]
        top, low = x[:32], x[32:]
        left = low_lanes(top)
        for side, block in enumerate((jnp.where(left, top, turned(low)), jnp.where(left, turned(top), low))):
            base = (2 * tile + side) * 64
            out_ref[base : base + 32, :] = block
            out_ref[base + 32 : base + 64, :] = gram


def packed(zs, own, got):
    return pl.pallas_call(
        lambda *refs: packing(zs, *refs),
        out_shape=jax.ShapeDtypeStruct((zs * 64, LANES), jnp.float32),
        compiler_params=pltpu.CompilerParams(vmem_limit_bytes=8 * MIB),
        name="packing",
    )(own, got)


def iterating(zs, members, got_ref, start_ref, out_ref):
    total = got_ref[0:64, :]
    for part in range(1, zs):
        total = total + got_ref[part * 64 : part * 64 + 64, :]
    target = unstack(total[:32])
    gram = unstack(total[32:])[:, :HALF]
    lip = jnp.max(jnp.sum(gram, axis=1, keepdims=True))
    factor = start_ref[...]
    ahead = factor
    momentum = 1.0
    for step in range(ITERS):
        slope = jnp.dot(
            gram, ahead, precision=lax.Precision.HIGHEST, preferred_element_type=jnp.float32
        ) - target
        fresh = jnp.maximum(ahead - slope / lip, 0.0)
        following = (1.0 + math.sqrt(1.0 + 4.0 * momentum * momentum)) / 2.0
        ahead = fresh + (momentum - 1.0) / following * (fresh - factor)
        factor = fresh
        momentum = following
    block = stack_sides(factor)
    for part in range(members):
        out_ref[part * 32 : part * 32 + 32, :] = block


def iterated(zs, members, got, start):
    return pl.pallas_call(
        lambda *refs: iterating(zs, members, *refs),
        out_shape=jax.ShapeDtypeStruct((members * 32, LANES), jnp.float32),
        compiler_params=pltpu.CompilerParams(vmem_limit_bytes=8 * MIB),
        name="iterating",
    )(got, start)


def fold_masks(shape):
    row = lax.broadcasted_iota(jnp.int32, shape, 0)
    lane = lax.broadcasted_iota(jnp.int32, shape, 1)
    row = row + jnp.where(lane < HALF, 0, 16)
    return lane % HALF < 32, row > lane % 32


def contracting(zs, got_ref, data_ref, factor_ref, out_ref, lines):
    width = zs * HALF
    for side in range(2):
        for pair in range(zs // 2):
            first, second = (2 * (2 * pair) + side) * 32, (2 * (2 * pair + 1) + side) * 32
            a = got_ref[first : first + 32, :]
            b = got_ref[second : second + 32, :]
            left = low_lanes(a)
            x = jnp.concatenate([jnp.where(left, a, turned(b)), jnp.where(left, turned(a), b)], axis=0)
            at = slice(side * width + pair * LANES, side * width + (pair + 1) * LANES)
            factor_ref[:, at] = x
            low = x.astype(jnp.bfloat16)
            lines[0:64, at] = low
            lines[64:128, at] = low
    factor = factor_ref[...]
    squares = jnp.sum(factor * factor, axis=1, keepdims=True)
    both = (((1,), (1,)), ((), ()))
    outer = lax.dot_general(lines[0:64, :], lines[...], both, preferred_element_type=jnp.float32)
    ones = jnp.ones((8, lines.shape[1]), jnp.bfloat16)
    sums = lax.dot_general(ones, lines[...], both, preferred_element_type=jnp.float32)[0:1, :]
    power = jnp.ceil(jnp.log(jnp.maximum(sums, 1e-30)) * LOG2E)
    power = jnp.clip(power, -60.0, 60.0)
    most = jnp.max(power, axis=1, keepdims=True)
    shrink = jnp.exp2(-power)
    row = lax.broadcasted_iota(jnp.int32, outer.shape, 0)
    lane = lax.broadcasted_iota(jnp.int32, outer.shape, 1)
    across = jnp.sum(jnp.where(row == lane % HALF, squares, 0.0), axis=0, keepdims=True)
    across = across * shrink * shrink * 32768.0
    wide = across * 8193.0
    high = wide - (wide - across)
    line = lax.broadcasted_iota(jnp.int32, (8, LANES), 0)
    extra = jnp.where(
        line == 0,
        jnp.where(low_lanes(high), high, across - high),
        jnp.where(line == 1, power, jnp.where(line == 2, power + most, 0.0)),
    )
    outer = outer * (shrink * jnp.exp2(-most) * 32768.0)
    top, low = outer[:32], outer[32:]
    lane = lax.broadcasted_iota(jnp.int32, top.shape, 1)
    row = lax.broadcasted_iota(jnp.int32, top.shape, 0)
    folded = jnp.where((lane % HALF < 32) & (row > lane % 32), pltpu.roll(low, 96, 1), top)
    folded = jnp.where(low_lanes(folded[:16]), folded[:16], folded[16:])
    shrink = shrink * 1024.0

    parts = data_ref.shape[0] // 64
    each = parts // BLOCKS
    for block in range(BLOCKS):
        at = slice(block * each * 64, (block + 1) * each * 64)
        terms = lax.dot_general(data_ref[at, :], lines[...], both, preferred_element_type=jnp.float32) * shrink
        for part in range(each):
            base = (block * each + part) * CHUNK
            out_ref[base : base + 32, :] = stack_copies(terms[part * 64 : part * 64 + 64])
            out_ref[base + 32 : base + 48, :] = folded
            out_ref[base + 48 : base + 56, :] = extra


def contracted(zs, got, data):
    rows, columns = data.shape
    return pl.pallas_call(
        lambda *refs: contracting(zs, *refs),
        out_shape=[
            jax.ShapeDtypeStruct((64, columns), jnp.float32),
            jax.ShapeDtypeStruct((rows // 64 * CHUNK, LANES), jnp.float32),
        ],
        in_specs=[pl.BlockSpec(memory_space=pltpu.VMEM)] * 2,
        out_specs=[pl.BlockSpec(memory_space=pltpu.VMEM)] * 2,
        scratch_shapes=[pltpu.VMEM((LANES, columns), jnp.bfloat16)],
        compiler_params=pltpu.CompilerParams(vmem_limit_bytes=16 * MIB),
        name="contracting",
    )(got, data)


def finishing(count, columns, got_ref, factor_ref, scaled_ref, gram_ref, terms_ref):
    folded_in, lower = fold_masks((16, LANES))
    swapped = folded_in & lower
    terms = jnp.zeros((32, LANES), jnp.float32)
    folded = jnp.zeros((16, LANES), jnp.float32)
    squares = jnp.zeros((1, LANES), jnp.float32)
    for part in range(count):
        base = part * CHUNK
        extra = got_ref[base + 48 : base + 56, :]
        grown = jnp.exp2(extra[1:3, :])
        grow, pair = grown[0:1], grown[1:2]
        terms = terms + got_ref[base : base + 32, :] * grow
        folded = folded + got_ref[base + 32 : base + 48, :] * jnp.where(swapped, pltpu.roll(pair, 96, 1), pair)
        squares = squares + (extra[0:1, :] + turned(extra[0:1, :])) * (grow * grow)
    squares = squares[:, :HALF] * (1.0 / 32768.0)
    upper = jnp.concatenate([folded, turned(folded)], axis=0) * (1.0 / 32768.0)
    upper = jnp.concatenate([upper, pltpu.roll(upper, 32, 1)], axis=0)
    mirror = jnp.transpose(upper)[:HALF, :]
    upper = upper[:, :HALF]
    row = lax.broadcasted_iota(jnp.int32, upper.shape, 0)
    lane = lax.broadcasted_iota(jnp.int32, upper.shape, 1)
    held = ((row < 32) & (row < lane)) | ((lane >= 32) & (row > lane))
    outer = jnp.where(row == lane, squares, jnp.where(held, upper, mirror))

    def scale_of(squares):
        mean = squares / columns + 1e-06
        first = lax.rsqrt(mean)
        return first * (1.5 - 0.5 * mean * first * first)

    across = scale_of(squares)
    down = scale_of(jnp.sum(jnp.where(row == lane, squares, 0.0), axis=1, keepdims=True))
    scaled_ref[...] = (factor_ref[...] * down).astype(jnp.bfloat16)
    gram_ref[...] = outer * down * across / columns
    terms = jnp.transpose(unstack(terms))[:HALF, :]
    terms_ref[...] = terms * down * (1.0 / 1024.0) / columns


def finished(count, columns, got, factor):
    return pl.pallas_call(
        lambda *refs: finishing(count, columns, *refs),
        out_shape=[
            jax.ShapeDtypeStruct(factor.shape, jnp.bfloat16),
            jax.ShapeDtypeStruct((64, 64), jnp.float32),
            jax.ShapeDtypeStruct((64, 64), jnp.float32),
        ],
        compiler_params=pltpu.CompilerParams(vmem_limit_bytes=8 * MIB),
        name="finishing",
    )(got, factor)


def shards(data, w_rows, h_init):
    members = lax.axis_size("row")
    zs = members // 2
    count = lax.axis_size("col")
    columns = data.shape[1] * count
    swap = [(2 * z + c, 2 * z + 1 - c) for z in range(zs) for c in range(2)]
    levels = [[2 * z + c for z in range(zs)] for c in range(2)]

    own, send, start = multiplied(zs, w_rows, data, h_init)
    got = lax.ppermute(send, "row", swap)
    parts = packed(zs, own, got)
    parts = lax.all_to_all(parts, "row", 0, 0, tiled=True, axis_index_groups=levels)
    copies = iterated(zs, members, parts, start)
    blocks = lax.all_to_all(copies, "row", 0, 0, tiled=True)
    factor, terms = contracted(zs, blocks, data)
    sums = lax.all_to_all(terms.astype(jnp.float16), "col", 0, 0, tiled=True)
    return tuple(finished(count, columns, sums.astype(jnp.float32), factor))


def solution(mesh):
    in_specs = (P("row", "col"), P(None, "row"), P(None, "col"))
    out_specs = (P(None, "col"), P(), P(None, ("row", "col")))
    return jax.shard_map(shards, mesh=mesh, in_specs=in_specs, out_specs=out_specs, check_vma=False)
```

time: 90.6 us -> 74.7 us (0.82); the launches traced: 88.8 us -> 74.5 us
  starting transfers between devices: 13.5 us -> 8.75 us
  blocking collectives: 61.8 us -> 57.2 us
  local copies, waits for them, and re-layouts: 4.09 us -> 0.01 us
  waiting for transfers between devices: 1.97 us -> 1.01 us
    ppermute x1 -> x0, starting transfers between devices: 4.72 us -> none  [shards(): other = lax.ppermute(mine, 'row', swap)]
    all_to_all x3, blocking collectives: 61.8 us -> 57.2 us  [the longest x1 25.7 us: shards(): sums = lax.all_to_all(terms.astype(jnp.float16), 'col', 0, 0, tiled=True)]
    unnamed x8 -> x2, local copies, waits for them, and re-layouts: 4.09 us -> 0.01 us
    ppermute x1 -> x0, waiting for transfers between devices: 0.96 us -> none  [shards(): other = lax.ppermute(mine, 'row', swap)]
  transfers between devices with their start and end apart: 2 -> 1, of which waited for: 2 -> 1; matrix products, arithmetic and copies ran while one was open for 0% -> 0% of each run, Pallas kernels for 0% -> 0%
where the time goes in v2:
time: 74.7 us; the launch traced here: 74.5 us
  blocking collectives  57.2 us (77%)
  starting transfers between devices  8.75 us (12%)
  Pallas kernels  6.63 us (9%)
  waiting for transfers between devices  1.01 us (1%)
    all_to_all x1, blocking collectives, shards(): sums = lax.all_to_all(terms.astype(jnp.float16), 'col', 0, 0, tiled=True)  25.7 us
    all_to_all x1, blocking collectives, shards(): blocks = lax.all_to_all(copies, 'row', 0, 0, tiled=True)  15.8 us
    all_to_all x1, blocking collectives, shards(): lax.all_to_all(parts, 'row', 0, 0, tiled=True, axis_index_groups=levels)  15.6 us
    ppermute x1, starting transfers between devices, shards(): got = lax.ppermute(send, 'row', swap)  8.75 us
    pallas_call x1, Pallas kernels, multiplied(): pl.pallas_call(lambda *refs: multiplying(zs, *refs), in_specs=[pl.BlockSp...  3.08 us
    pallas_call x1, Pallas kernels, contracted(): pl.pallas_call(lambda *refs: contracting(zs, *refs), out_shape=[jax.Shape...  1.5 us
  transfers between devices with their start and end apart: 1, of which 1 were waited for; matrix products, arithmetic and copies ran while one was open for 0% of the time, Pallas kernels for 0%

profile of v2, /device:TPU:1, one launch (start us, length us, event | category | flops | bytes accessed | tf_op | source)
XLA Modules:
  0.0 74.5 jit_solution(10144628296911259553)
XLA Ops:
  0.6 0.0 copy-start
  0.6 3.1 %multiplying.1 = (f32[64,640]{1,0:T(8,128)S(1)}, f32[64,640]{1,0:T(8,128)S(1)}, f32[64,128]{1,0:T(8,128)S(1)}) custom-call(bf16[64,2048]{1,0:T(8,128)(2,1)} %refs_0_.1, bf16[2048,1024]{1,0:T(8,128)(2,1)} %refs_1_.3, f32[64,1024]{1,0:T(8,128)} %refs_2_.1), custom_call_target="tpu_custom_call" | custom-call | tf_op jit(solution)/shard_map/multiplying/pallas_call | solution.py:86
  3.7 8.7 %collective-permute-start = (f32[64,640]{1,0:T(8,128)S(1)}, f32[64,640]{1,0:T(8,128)S(1)}, u32[]{:S(2)}, u32[]{:S(2)}) collective-permute-start(f32[64,640]{1,0:T(8,128)S(1)} %get-tuple-element.9), channel_id=1, source_target_pairs={{0,32},{32,0},{64,96},{96,64},{128,160},{160,128},{192,224},{224,1... | collective-permute-start | bytes 491528 | tf_op jit(solution)/shard_map/ppermute | solution.py:297
  12.5 1.0 %collective-permute-done.refs_1_ = f32[64,640]{1,0:T(8,128)S(1)} collective-permute-done((f32[64,640]{1,0:T(8,128)S(1)}, f32[64,640]{1,0:T(8,128)S(1)}, u32[]{:S(2)}, u32[]{:S(2)}) %collective-permute-start) | collective-permute-done | bytes 163872 | tf_op jit(solution)/shard_map/ppermute | solution.py:297
  13.5 0.1 packing.1
  13.6 15.6 %all_to_all.31 = f32[8,64,128]{2,1,0:T(8,128)S(1)} all-to-all(f32[8,64,128]{2,1,0:T(8,128)S(1)} %bitcast.10), channel_id=1, replica_groups={{0,64,128,192,256,320,384,448},{32,96,160,224,288,352,416,480},{1,65,12..., dimensions={0} | all-to-all | bytes 524288 | tf_op jit(solution)/shard_map/all_to_all | solution.py:299
  29.2 0.9 %iterating.1 = f32[512,128]{1,0:T(8,128)S(1)} custom-call(f32[512,128]{1,0:T(8,128)S(1)} %bitcast.9, f32[64,128]{1,0:T(8,128)S(1)} %get-tuple-element.10.refs_1_), custom_call_target="tpu_custom_call" | custom-call | tf_op jit(solution)/shard_map/iterating/pallas_call | solution.py:151
  30.1 15.8 %all_to_all.32 = f32[16,32,128]{2,1,0:T(8,128)S(1)} all-to-all(f32[16,32,128]{2,1,0:T(8,128)S(1)} %bitcast.11), channel_id=1, replica_groups=mesh['row'=16,'col'=32] {'row'}, dimensions={0} | all-to-all | bytes 524288 | tf_op jit(solution)/shard_map/all_to_all | solution.py:301
  45.9 0.0 copy-done
  46.0 1.5 %contracting.1 = (f32[64,1024]{1,0:T(8,128)S(1)}, f32[1792,128]{1,0:T(8,128)S(1)}) custom-call(f32[512,128]{1,0:T(8,128)S(1)} %bitcast.8, bf16[2048,1024]{1,0:T(8,128)(2,1)S(1)} %copy-done), custom_call_target="tpu_custom_call" | custom-call | tf_op jit(solution)/shard_map/contracting/pallas_call | solution.py:224
  47.5 0.1 convert_element_type.8
  47.5 25.7 %all_to_all.33 = f16[32,56,128]{2,1,0:T(8,128)(2,1)S(1)} all-to-all(f16[32,56,128]{2,1,0:T(8,128)(2,1)S(1)} %bitcast.12), channel_id=1, replica_groups=mesh['row'=16,'col'=32] {'col'}, dimensions={0} | all-to-all | bytes 917504 | tf_op jit(solution)/shard_map/all_to_all | solution.py:303
  73.3 0.1 bitcast_convert_fusion.refs_0_
  73.4 1.1 %finishing.1 = (bf16[64,1024]{1,0:T(8,128)(2,1)}, f32[64,64]{1,0:T(8,128)}, f32[64,64]{1,0:T(8,128)}) custom-call(f32[1792,128]{1,0:T(8,128)S(1)} %bitcast_convert_fusion.refs_0_, f32[64,1024]{1,0:T(8,128)S(1)} %get-tuple-element.12.refs_1_), custom_call_target="tpu_custom_call" | custom-call | tf_op jit(solution)/shard_map/finishing/pallas_call | solution.py:276
Async XLA Ops:
  0.6 45.3 %copy-start = (bf16[2048,1024]{1,0:T(8,128)(2,1)S(1)}, bf16[2048,1024]{1,0:T(8,128)(2,1)}, u32[]{:S(2)}) copy-start(bf16[2048,1024]{1,0:T(8,128)(2,1)} %refs_1_.3) | copy-start | bytes 12582916
  3.7 9.8 %collective-permute-start = (f32[64,640]{1,0:T(8,128)S(1)}, f32[64,640]{1,0:T(8,128)S(1)}, u32[]{:S(2)}, u32[]{:S(2)}) collective-permute-start(f32[64,640]{1,0:T(8,128)S(1)} %get-tuple-element.9), channel_id=1, source_target_pairs={{0,32},{32,0},{64,96},{96,64},{128,160},{160,128},{192,224},{224,1... | collective-permute-start | bytes 491528 | tf_op jit(solution)/shard_map/ppermute | solution.py:297

commit v3 on v2

--- a/solution.py
+++ b/solution.py
@@ -12,6 +12,7 @@
 LANES = 128
 HALF = 64
 BLOCKS = 4
+GRANT = 55947264
 CHUNK = 56
 MIB = 1 << 20
 
@@ -36,73 +37,88 @@
     return jnp.concatenate([x, turned(x)], axis=0)
 
 
-def multiplying(zs, w_hbm, data_hbm, h_hbm, own_ref, send_ref, start_ref, data_ref, w, h, acc, sems):
-    rows, columns = data_ref.shape
-    width = columns // 2
+def sending(w_hbm, data_hbm, h_hbm, send_ref, start_ref, w, data_ref, h, acc, sems):
+    rows, width = data_ref.shape
     depth = rows // BLOCKS
     me = lax.axis_index("row")
     core, level = lax.rem(me, 2), lax.div(me, 2)
+    theirs = pl.multiple_of((1 - core) * width, LANES)
     tile = core * (width // LANES) + lax.div(level, 2)
-    copies = [
-        pltpu.make_async_copy(w_hbm, w, sems.at[BLOCKS]),
+    copies = [pltpu.make_async_copy(w_hbm, w, sems.at[BLOCKS])]
+    for block in range(BLOCKS):
+        at = pl.ds(block * depth, depth)
+        copies.append(
+            pltpu.make_async_copy(data_hbm.at[at, pl.ds(theirs, width)], data_ref.at[at, :], sems.at[block])
+        )
+    copies.append(
         pltpu.make_async_copy(
             h_hbm.at[:, pl.ds(pl.multiple_of(tile * LANES, LANES), LANES)], h, sems.at[BLOCKS + 1]
-        ),
-    ]
-    for block in range(BLOCKS):
-        at = pl.ds(block * depth, depth)
-        copies.append(pltpu.make_async_copy(data_hbm.at[at, :], data_ref.at[at, :], sems.at[block]))
-    for copy in (copies[0], *copies[2:], copies[1]):
+        )
+    )
+    for copy in copies:
         copy.start()
     copies[0].wait()
-    gram = lax.dot_general(
+    send_ref[:, width:] = lax.dot_general(
         w[...], jnp.concatenate([w[...], w[...]], axis=0), (((1,), (1,)), ((), ())), preferred_element_type=jnp.float32
     )
-    own_ref[:, width:] = gram
-    send_ref[:, width:] = gram
     for block in range(BLOCKS):
-        copies[2 + block].wait()
+        copies[1 + block].wait()
         at = slice(block * depth, (block + 1) * depth)
         part = jnp.dot(w[:, at], data_ref[at, :], preferred_element_type=jnp.float32)
         if block == 0:
             acc[...] = part
+        elif block < BLOCKS - 1:
+            acc[...] += part
         else:
-            acc[...] += part
-    first = core == 0
-    left = acc[:, :width]
-    right = acc[:, width:]
-    own_ref[:, :width] = jnp.where(first, left, right)
-    send_ref[:, :width] = jnp.where(first, right, left)
-    copies[1].wait()
+            send_ref[:, :width] = acc[...] + part
+    copies[BLOCKS + 1].wait()
     begin = h[...]
     start_ref[...] = jnp.where(lax.rem(level, 2) == 0, begin, turned(begin))
 
 
-def multiplied(zs, w_rows, data, h_init):
+def sent(w_rows, data, h_init):
     rows, columns = data.shape
-    rank = w_rows.shape[0]
-    half = jax.ShapeDtypeStruct((rank, columns // 2 + LANES), jnp.float32)
-    start = jax.ShapeDtypeStruct((rank, LANES), jnp.float32)
-    return pl.pallas_call(
-        lambda *refs: multiplying(zs, *refs),
+    rank, width = w_rows.shape[0], columns // 2
+    return pl.pallas_call(
+        sending,
         in_specs=[pl.BlockSpec(memory_space=pl.ANY)] * 3,
         out_specs=[pl.BlockSpec(memory_space=pltpu.VMEM)] * 3,
-        out_shape=[half, half, start],
+        out_shape=[
+            jax.ShapeDtypeStruct((rank, width + LANES), jnp.float32),
+            jax.ShapeDtypeStruct((rank, LANES), jnp.float32),
+            jax.ShapeDtypeStruct(w_rows.shape, w_rows.dtype),
+        ],
         scratch_shapes=[
-            pltpu.VMEM(data.shape, data.dtype),
-            pltpu.VMEM(w_rows.shape, w_rows.dtype),
+            pltpu.VMEM((rows, width), data.dtype),
             pltpu.VMEM((rank, LANES), jnp.float32),
-            pltpu.VMEM((rank, columns), jnp.float32),
+            pltpu.VMEM((rank, width), jnp.float32),
             pltpu.SemaphoreType.DMA((BLOCKS + 2,)),
         ],
-        compiler_params=pltpu.CompilerParams(vmem_limit_bytes=56045568),
-        name="multiplying",
+        compiler_params=pltpu.CompilerParams(vmem_limit_bytes=GRANT),
+        name="sending",
     )(w_rows, data, h_init)
 
 
-def packing(zs, own_ref, got_ref, out_ref):
-    width = own_ref.shape[1] - LANES
-    gram = stack_copies(own_ref[:, width:] + got_ref[:, width:])
+def keeping(w_ref, data_ref, own_ref):
+    width = own_ref.shape[1]
+    mine = pl.multiple_of(lax.rem(lax.axis_index("row"), 2) * width, LANES)
+    own_ref[...] = jnp.dot(w_ref[...], data_ref[:, pl.ds(mine, width)], preferred_element_type=jnp.float32)
+
+
+def kept(w_rows, data):
+    return pl.pallas_call(
+        keeping,
+        in_specs=[pl.BlockSpec(memory_space=pltpu.VMEM)] * 2,
+        out_specs=pl.BlockSpec(memory_space=pltpu.VMEM),
+        out_shape=jax.ShapeDtypeStruct((w_rows.shape[0], data.shape[1] // 2), jnp.float32),
+        compiler_params=pltpu.CompilerParams(vmem_limit_bytes=8 * MIB),
+        name="keeping",
+    )(w_rows, data)
+
+
+def packing(zs, own_ref, send_ref, got_ref, out_ref):
+    width = own_ref.shape[1]
+    gram = stack_copies(send_ref[:, width:] + got_ref[:, width:])
     for tile in range(width // LANES):
         at = slice(tile * LANES, (tile + 1) * LANES)
         x = own_ref[:, at] + got_ref[:, at]
@@ -114,13 +130,13 @@
             out_ref[base + 32 : base + 64, :] = gram
 
 
-def packed(zs, own, got):
+def packed(zs, own, send, got):
     return pl.pallas_call(
         lambda *refs: packing(zs, *refs),
         out_shape=jax.ShapeDtypeStruct((zs * 64, LANES), jnp.float32),
         compiler_params=pltpu.CompilerParams(vmem_limit_bytes=8 * MIB),
         name="packing",
-    )(own, got)
+    )(own, send, got)
 
 
 def iterating(zs, members, got_ref, start_ref, out_ref):
@@ -163,26 +179,71 @@
     return lane % HALF < 32, row > lane % 32
 
 
-def contracting(zs, got_ref, data_ref, factor_ref, out_ref, lines):
+BOTH = (((1,), (1,)), ((), ()))
+
+
+def unpacking(zs, got_ref):
+    for pair in range(zs // 2):
+        a = got_ref[pair * 64 : pair * 64 + 32, :]
+        b = got_ref[pair * 64 + 32 : pair * 64 + 64, :]
+        left = low_lanes(a)
+        yield jnp.concatenate([jnp.where(left, a, turned(b)), jnp.where(left, turned(a), b)], axis=0)
+
+
+def starting(zs, got_ref, data_ref, factor_ref, terms_ref, lines):
     width = zs * HALF
-    for side in range(2):
-        for pair in range(zs // 2):
-            first, second = (2 * (2 * pair) + side) * 32, (2 * (2 * pair + 1) + side) * 32
-            a = got_ref[first : first + 32, :]
-            b = got_ref[second : second + 32, :]
-            left = low_lanes(a)
-            x = jnp.concatenate([jnp.where(left, a, turned(b)), jnp.where(left, turned(a), b)], axis=0)
-            at = slice(side * width + pair * LANES, side * width + (pair + 1) * LANES)
-            factor_ref[:, at] = x
-            low = x.astype(jnp.bfloat16)
-            lines[0:64, at] = low
-            lines[64:128, at] = low
+    mine = pl.multiple_of(lax.rem(lax.axis_index("row"), 2) * width, LANES)
+    for pair, x in enumerate(unpacking(zs, got_ref)):
+        at = slice(pair * LANES, (pair + 1) * LANES)
+        factor_ref[:, at] = x
+        low = x.astype(jnp.bfloat16)
+        lines[0:64, at] = low
+        lines[64:128, at] = low
+    step = data_ref.shape[0] // BLOCKS
+    for block in range(BLOCKS):
+        at = slice(block * step, (block + 1) * step)
+        terms_ref[at, :] = lax.dot_general(
+            data_ref[at, pl.ds(mine, width)], lines[...], BOTH, preferred_element_type=jnp.float32
+        )
+
+
+def started(zs, got, data):
+    width = zs * HALF
+    return pl.pallas_call(
+        lambda *refs: starting(zs, *refs),
+        out_shape=[
+            jax.ShapeDtypeStruct((64, width), jnp.float32),
+            jax.ShapeDtypeStruct((data.shape[0], LANES), jnp.float32),
+        ],
+        in_specs=[pl.BlockSpec(memory_space=pltpu.VMEM)] * 2,
+        out_specs=[pl.BlockSpec(memory_space=pltpu.VMEM)] * 2,
+        scratch_shapes=[pltpu.VMEM((LANES, width), jnp.bfloat16)],
+        compiler_params=pltpu.CompilerParams(vmem_limit_bytes=8 * MIB),
+        name="starting",
+    )(got, data)
+
+
+def contracting(zs, got_ref, half_ref, begun_ref, data_ref, factor_ref, out_ref, lines):
+    width = zs * HALF
+    core = lax.rem(lax.axis_index("row"), 2)
+    mine = pl.multiple_of(core * width, LANES)
+    theirs = pl.multiple_of((1 - core) * width, LANES)
+    half = half_ref[...]
+    factor_ref[:, pl.ds(mine, width)] = half
+    for pair, x in enumerate(unpacking(zs, got_ref)):
+        at = slice(pair * LANES, (pair + 1) * LANES)
+        factor_ref[:, pl.ds(pl.multiple_of(theirs + pair * LANES, LANES), LANES)] = x
+        low = x.astype(jnp.bfloat16)
+        lines[0:64, at] = low
+        lines[64:128, at] = low
+    low = half.astype(jnp.bfloat16)
+    lines[0:64, width:] = low
+    lines[64:128, width:] = low
     factor = factor_ref[...]
     squares = jnp.sum(factor * factor, axis=1, keepdims=True)
-    both = (((1,), (1,)), ((), ()))
-    outer = lax.dot_general(lines[0:64, :], lines[...], both, preferred_element_type=jnp.float32)
+    outer = lax.dot_general(lines[0:64, :], lines[...], BOTH, preferred_element_type=jnp.float32)
     ones = jnp.ones((8, lines.shape[1]), jnp.bfloat16)
-    sums = lax.dot_general(ones, lines[...], both, preferred_element_type=jnp.float32)[0:1, :]
+    sums = lax.dot_general(ones, lines[...], BOTH, preferred_element_type=jnp.float32)[0:1, :]
     power = jnp.ceil(jnp.log(jnp.maximum(sums, 1e-30)) * LOG2E)
     power = jnp.clip(power, -60.0, 60.0)
     most = jnp.max(power, axis=1, keepdims=True)
@@ -211,7 +272,10 @@
     each = parts // BLOCKS
     for block in range(BLOCKS):
         at = slice(block * each * 64, (block + 1) * each * 64)
-        terms = lax.dot_general(data_ref[at, :], lines[...], both, preferred_element_type=jnp.float32) * shrink
+        terms = lax.dot_general(
+            data_ref[at, pl.ds(theirs, width)], lines[:, :width], BOTH, preferred_element_type=jnp.float32
+        )
+        terms = (terms + begun_ref[at, :]) * shrink
         for part in range(each):
             base = (block * each + part) * CHUNK
             out_ref[base : base + 32, :] = stack_copies(terms[part * 64 : part * 64 + 64])
@@ -219,7 +283,7 @@
             out_ref[base + 48 : base + 56, :] = extra
 
 
-def contracted(zs, got, data):
+def contracted(zs, got, half, begun, data):
     rows, columns = data.shape
     return pl.pallas_call(
         lambda *refs: contracting(zs, *refs),
@@ -227,12 +291,12 @@
             jax.ShapeDtypeStruct((64, columns), jnp.float32),
             jax.ShapeDtypeStruct((rows // 64 * CHUNK, LANES), jnp.float32),
         ],
-        in_specs=[pl.BlockSpec(memory_space=pltpu.VMEM)] * 2,
+        in_specs=[pl.BlockSpec(memory_space=pltpu.VMEM)] * 4,
         out_specs=[pl.BlockSpec(memory_space=pltpu.VMEM)] * 2,
         scratch_shapes=[pltpu.VMEM((LANES, columns), jnp.bfloat16)],
         compiler_params=pltpu.CompilerParams(vmem_limit_bytes=16 * MIB),
         name="contracting",
-    )(got, data)
+    )(got, half, begun, data)
 
 
 def finishing(count, columns, got_ref, factor_ref, scaled_ref, gram_ref, terms_ref):
@@ -293,13 +357,16 @@
     swap = [(2 * z + c, 2 * z + 1 - c) for z in range(zs) for c in range(2)]
     levels = [[2 * z + c for z in range(zs)] for c in range(2)]
 
-    own, send, start = multiplied(zs, w_rows, data, h_init)
+    send, start, w_rows = sent(w_rows, data, h_init)
     got = lax.ppermute(send, "row", swap)
-    parts = packed(zs, own, got)
+    own = kept(w_rows, data)
+    parts = packed(zs, own, send, got)
     parts = lax.all_to_all(parts, "row", 0, 0, tiled=True, axis_index_groups=levels)
-    copies = iterated(zs, members, parts, start)
-    blocks = lax.all_to_all(copies, "row", 0, 0, tiled=True)
-    factor, terms = contracted(zs, blocks, data)
+    copies = iterated(zs, zs, parts, start)
+    blocks = lax.all_to_all(copies, "row", 0, 0, tiled=True, axis_index_groups=levels)
+    others = lax.ppermute(blocks, "row", swap)
+    half, begun = started(zs, blocks, data)
+    factor, terms = contracted(zs, others, half, begun, data)
     sums = lax.all_to_all(terms.astype(jnp.float16), "col", 0, 0, tiled=True)
     return tuple(finished(count, columns, sums.astype(jnp.float32), factor))
 

time: 74.7 us -> 73.1 us (0.979)
  blocking collectives: 57.2 us -> 50.9 us
  starting transfers between devices: 8.75 us -> 13.5 us
    all_to_all x1, blocking collectives: 15.8 us -> 10.3 us  [shards(): lax.all_to_all(copies, 'row', 0, 0, tiled=True, axis_index_groups=levels)]
    ppermute x0 -> x1, starting transfers between devices: none -> 4.73 us  [shards(): others = lax.ppermute(blocks, 'row', swap)]
    all_to_all x1, blocking collectives: 25.7 us -> 25 us  [shards(): sums = lax.all_to_all(terms.astype(jnp.float16), 'col', 0, 0, tiled=True)]
    pallas_call x1 -> x3, Pallas kernels: 3.08 us -> 3.79 us  [the longest x1 2.51 us: sent(): pl.pallas_call(sending, in_specs=[pl.BlockSpec(memory_space=pl.ANY)] * 3,...]
  transfers between devices with their start and end apart: 1 -> 2, of which waited for: 1 -> 2; matrix products, arithmetic and copies ran while one was open for 0% -> 0% of each run, Pallas kernels for 0% -> 2%
where the time goes in v3:
time: 73.1 us; the launch traced here: 72.8 us
  blocking collectives  50.9 us (70%)
  starting transfers between devices  13.5 us (18%)
  Pallas kernels  6.81 us (9%)
    all_to_all x1, blocking collectives, shards(): sums = lax.all_to_all(terms.astype(jnp.float16), 'col', 0, 0, tiled=True)  25 us
    all_to_all x1, blocking collectives, shards(): lax.all_to_all(parts, 'row', 0, 0, tiled=True, axis_index_groups=levels)  15.6 us
    all_to_all x1, blocking collectives, shards(): lax.all_to_all(copies, 'row', 0, 0, tiled=True, axis_index_groups=levels)  10.3 us
    ppermute x1, starting transfers between devices, shards(): got = lax.ppermute(send, 'row', swap)  8.75 us
    ppermute x1, starting transfers between devices, shards(): others = lax.ppermute(blocks, 'row', swap)  4.73 us
    pallas_call x1, Pallas kernels, sent(): pl.pallas_call(sending, in_specs=[pl.BlockSpec(memory_space=pl.ANY)] * 3,...  2.51 us
  transfers between devices with their start and end apart: 2, of which 2 were waited for; matrix products, arithmetic and copies ran while one was open for 0% of the time, Pallas kernels for 2%

profile of v3, /device:TPU:1, one launch (start us, length us, event | category | flops | bytes accessed | tf_op | source)
XLA Modules:
  0.0 72.8 jit_solution(12504562300678878045)
XLA Ops:
  0.6 0.0 copy-start
  0.6 2.5 %sending.1 = (f32[64,640]{1,0:T(8,128)S(1)}, f32[64,128]{1,0:T(8,128)S(1)}, bf16[64,2048]{1,0:T(8,128)(2,1)S(1)}) custom-call(bf16[64,2048]{1,0:T(8,128)(2,1)} %w_hbm.1, bf16[2048,1024]{1,0:T(8,128)(2,1)} %refs_3_.1, f32[64,1024]{1,0:T(8,128)} %h_hbm.1), custom_call_target="tpu_custom_call" | custom-call | tf_op jit(solution)/shard_map/sending/pallas_call | solution.py:82
  3.2 8.8 %collective-permute-start = (f32[64,640]{1,0:T(8,128)S(1)}, f32[64,640]{1,0:T(8,128)S(1)}, u32[]{:S(2)}, u32[]{:S(2)}) collective-permute-start(f32[64,640]{1,0:T(8,128)S(1)} %get-tuple-element.11.refs_1_), channel_id=1, source_target_pairs={{0,32},{32,0},{64,96},{96,64},{128,160},{160,128},{192,224},{224,1... | collective-permute-start | bytes 491528 | tf_op jit(solution)/shard_map/ppermute | solution.py:361
  11.9 0.0 copy-done
  11.9 0.5 keeping.1.refs_0_
  12.4 0.5 collective-permute-done.refs_2_
  12.9 0.1 packing.1
  13.0 15.6 %all_to_all.31 = f32[8,64,128]{2,1,0:T(8,128)S(1)} all-to-all(f32[8,64,128]{2,1,0:T(8,128)S(1)} %bitcast.9), channel_id=1, replica_groups={{0,64,128,192,256,320,384,448},{32,96,160,224,288,352,416,480},{1,65,12..., dimensions={0} | all-to-all | bytes 524288 | tf_op jit(solution)/shard_map/all_to_all | solution.py:364
  28.7 0.8 %iterating.1 = f32[256,128]{1,0:T(8,128)S(1)} custom-call(f32[512,128]{1,0:T(8,128)S(1)} %bitcast.8, f32[64,128]{1,0:T(8,128)S(1)} %get-tuple-element.12.refs_1_), custom_call_target="tpu_custom_call" | custom-call | tf_op jit(solution)/shard_map/iterating/pallas_call | solution.py:167
  29.5 10.3 %all_to_all.32 = f32[8,32,128]{2,1,0:T(8,128)S(1)} all-to-all(f32[8,32,128]{2,1,0:T(8,128)S(1)} %bitcast.12), channel_id=1, replica_groups={{0,64,128,192,256,320,384,448},{32,96,160,224,288,352,416,480},{1,65,12..., dimensions={0} | all-to-all | bytes 262144 | tf_op jit(solution)/shard_map/all_to_all | solution.py:366
  39.8 4.7 %collective-permute-start.1 = (f32[256,128]{1,0:T(8,128)S(1)}, f32[256,128]{1,0:T(8,128)S(1)}, u32[]{:S(2)}, u32[]{:S(2)}) collective-permute-start(f32[256,128]{1,0:T(8,128)S(1)} %bitcast.10), channel_id=1, source_target_pairs={{0,32},{32,0},{64,96},{96,64},{128,160},{160,128},{192,224},{224,1... | collective-permute-start | bytes 393224 | tf_op jit(solution)/shard_map/ppermute | solution.py:367
  44.6 0.8 %starting.1 = (f32[64,512]{1,0:T(8,128)S(1)}, f32[2048,128]{1,0:T(8,128)S(1)}) custom-call(f32[256,128]{1,0:T(8,128)S(1)} %bitcast.11, bf16[2048,1024]{1,0:T(8,128)(2,1)S(1)} %copy-done), custom_call_target="tpu_custom_call" | custom-call | tf_op jit(solution)/shard_map/starting/pallas_call | solution.py:212
  45.4 0.2 collective-permute-done.1.refs_0_
  45.5 1.0 %contracting.1 = (f32[64,1024]{1,0:T(8,128)S(1)}, f32[1792,128]{1,0:T(8,128)S(1)}) custom-call(f32[256,128]{1,0:T(8,128)S(1)} %collective-permute-done.1.refs_0_, f32[64,512]{1,0:T(8,128)S(1)} %get-tuple-element.13.refs_1_, f32[2048,128]{1,0:T(8,128)S(1)} %get-tuple-element.14.refs_2_, bf16[2048,1024]{1,0:T(8,128)(2,1)S(1)} %copy-done), custom_call_target="tpu_custom_call" | custom-call | tf_op jit(solution)/shard_map/contracting/pallas_call | solution.py:288
  46.5 0.1 convert_element_type.8
  46.6 25.0 %all_to_all.33 = f16[32,56,128]{2,1,0:T(8,128)(2,1)S(1)} all-to-all(f16[32,56,128]{2,1,0:T(8,128)(2,1)S(1)} %bitcast.13), channel_id=1, replica_groups=mesh['row'=16,'col'=32] {'col'}, dimensions={0} | all-to-all | bytes 917504 | tf_op jit(solution)/shard_map/all_to_all | solution.py:370
  71.6 0.1 bitcast_convert_fusion.refs_0_
  71.7 1.1 %finishing.1 = (bf16[64,1024]{1,0:T(8,128)(2,1)}, f32[64,64]{1,0:T(8,128)}, f32[64,64]{1,0:T(8,128)}) custom-call(f32[1792,128]{1,0:T(8,128)S(1)} %bitcast_convert_fusion.refs_0_, f32[64,1024]{1,0:T(8,128)S(1)} %get-tuple-element.16.refs_1_), custom_call_target="tpu_custom_call" | custom-call | tf_op jit(solution)/shard_map/finishing/pallas_call | solution.py:340
Async XLA Ops:
  0.6 11.3 %copy-start = (bf16[2048,1024]{1,0:T(8,128)(2,1)S(1)}, bf16[2048,1024]{1,0:T(8,128)(2,1)}, u32[]{:S(2)}) copy-start(bf16[2048,1024]{1,0:T(8,128)(2,1)} %refs_3_.1) | copy-start | bytes 12582916
  3.2 9.8 %collective-permute-start = (f32[64,640]{1,0:T(8,128)S(1)}, f32[64,640]{1,0:T(8,128)S(1)}, u32[]{:S(2)}, u32[]{:S(2)}) collective-permute-start(f32[64,640]{1,0:T(8,128)S(1)} %get-tuple-element.11.refs_1_), channel_id=1, source_target_pairs={{0,32},{32,0},{64,96},{96,64},{128,160},{160,128},{192,224},{224,1... | collective-permute-start | bytes 491528 | tf_op jit(solution)/shard_map/ppermute | solution.py:361
  39.8 5.7 %collective-permute-start.1 = (f32[256,128]{1,0:T(8,128)S(1)}, f32[256,128]{1,0:T(8,128)S(1)}, u32[]{:S(2)}, u32[]{:S(2)}) collective-permute-start(f32[256,128]{1,0:T(8,128)S(1)} %bitcast.10), channel_id=1, source_target_pairs={{0,32},{32,0},{64,96},{96,64},{128,160},{160,128},{192,224},{224,1... | collective-permute-start | bytes 393224 | tf_op jit(solution)/shard_map/ppermute | solution.py:367

commit v4 on v2

--- a/solution.py
+++ b/solution.py
@@ -102,10 +102,12 @@
 
 def packing(zs, own_ref, got_ref, out_ref):
     width = own_ref.shape[1] - LANES
-    gram = stack_copies(own_ref[:, width:] + got_ref[:, width:])
+    rank = own_ref.shape[0]
+    theirs = pl.ds(pl.multiple_of((1 - lax.rem(lax.axis_index("row"), 2)) * rank, 8), rank)
+    gram = stack_copies(own_ref[:, width:] + got_ref[theirs, width:])
     for tile in range(width // LANES):
         at = slice(tile * LANES, (tile + 1) * LANES)
-        x = own_ref[:, at] + got_ref[:, at]
+        x = own_ref[:, at] + got_ref[theirs, at]
         top, low = x[:32], x[32:]
         left = low_lanes(top)
         for side, block in enumerate((jnp.where(left, top, turned(low)), jnp.where(left, turned(top), low))):
@@ -123,7 +125,7 @@
     )(own, got)
 
 
-def iterating(zs, members, got_ref, start_ref, out_ref):
+def iterating(zs, got_ref, start_ref, out_ref):
     total = got_ref[0:64, :]
     for part in range(1, zs):
         total = total + got_ref[part * 64 : part * 64 + 64, :]
@@ -143,14 +145,14 @@
         factor = fresh
         momentum = following
     block = stack_sides(factor)
-    for part in range(members):
+    for part in range(zs):
         out_ref[part * 32 : part * 32 + 32, :] = block
 
 
-def iterated(zs, members, got, start):
-    return pl.pallas_call(
-        lambda *refs: iterating(zs, members, *refs),
-        out_shape=jax.ShapeDtypeStruct((members * 32, LANES), jnp.float32),
+def iterated(zs, got, start):
+    return pl.pallas_call(
+        lambda *refs: iterating(zs, *refs),
+        out_shape=jax.ShapeDtypeStruct((zs * 32, LANES), jnp.float32),
         compiler_params=pltpu.CompilerParams(vmem_limit_bytes=8 * MIB),
         name="iterating",
     )(got, start)
@@ -167,7 +169,8 @@
     width = zs * HALF
     for side in range(2):
         for pair in range(zs // 2):
-            first, second = (2 * (2 * pair) + side) * 32, (2 * (2 * pair + 1) + side) * 32
+            first = (side * zs + 2 * pair) * 32
+            second = first + 32
             a = got_ref[first : first + 32, :]
             b = got_ref[second : second + 32, :]
             left = low_lanes(a)
@@ -290,15 +293,16 @@
     zs = members // 2
     count = lax.axis_size("col")
     columns = data.shape[1] * count
-    swap = [(2 * z + c, 2 * z + 1 - c) for z in range(zs) for c in range(2)]
+    pairs = [[2 * z + c for c in range(2)] for z in range(zs)]
     levels = [[2 * z + c for z in range(zs)] for c in range(2)]
 
     own, send, start = multiplied(zs, w_rows, data, h_init)
-    got = lax.ppermute(send, "row", swap)
+    got = lax.all_gather(send, "row", axis=0, tiled=True, axis_index_groups=pairs)
     parts = packed(zs, own, got)
     parts = lax.all_to_all(parts, "row", 0, 0, tiled=True, axis_index_groups=levels)
-    copies = iterated(zs, members, parts, start)
-    blocks = lax.all_to_all(copies, "row", 0, 0, tiled=True)
+    copies = iterated(zs, parts, start)
+    blocks = lax.all_to_all(copies, "row", 0, 0, tiled=True, axis_index_groups=levels)
+    blocks = lax.all_gather(blocks, "row", axis=0, tiled=True, axis_index_groups=pairs)
     factor, terms = contracted(zs, blocks, data)
     sums = lax.all_to_all(terms.astype(jnp.float16), "col", 0, 0, tiled=True)
     return tuple(finished(count, columns, sums.astype(jnp.float32), factor))

time: 74.7 us -> 71.6 us (0.959)
  starting transfers between devices: 8.75 us -> 0 us
  blocking collectives: 57.2 us -> 63.9 us
  waiting for transfers between devices: 1.01 us -> 0 us
    all_gather x0 -> x2, blocking collectives: none -> 13 us  [the longest x1 8.51 us: shards(): lax.all_gather(send, 'row', axis=0, tiled=True, axis_index_groups=pairs)]
    ppermute x1 -> x0, starting transfers between devices: 8.75 us -> none  [shards(): got = lax.ppermute(send, 'row', swap)]
    all_to_all x1, blocking collectives: 15.8 us -> 10.3 us  [shards(): lax.all_to_all(copies, 'row', 0, 0, tiled=True, axis_index_groups=levels)]
    ppermute x1 -> x0, waiting for transfers between devices: 1.01 us -> none  [shards(): got = lax.ppermute(send, 'row', swap)]
    all_to_all x1, blocking collectives: 25.7 us -> 25 us  [shards(): sums = lax.all_to_all(terms.astype(jnp.float16), 'col', 0, 0, tiled=True)]
  transfers between devices with their start and end apart: 1 -> 0, of which waited for: 1 -> 0; matrix products, arithmetic and copies ran while one was open for 0% -> 0% of each run, Pallas kernels for 0% -> 0%
where the time goes in v4:
time: 71.6 us; the launch traced here: 71.3 us
  blocking collectives  63.9 us (89%)
  Pallas kernels  6.62 us (9%)
    all_to_all x1, blocking collectives, shards(): sums = lax.all_to_all(terms.astype(jnp.float16), 'col', 0, 0, tiled=True)  25 us
    all_to_all x1, blocking collectives, shards(): lax.all_to_all(parts, 'row', 0, 0, tiled=True, axis_index_groups=levels)  15.6 us
    all_to_all x1, blocking collectives, shards(): lax.all_to_all(copies, 'row', 0, 0, tiled=True, axis_index_groups=levels)  10.3 us
    all_gather x1, blocking collectives, shards(): lax.all_gather(send, 'row', axis=0, tiled=True, axis_index_groups=pairs)  8.51 us
    all_gather x1, blocking collectives, shards(): lax.all_gather(blocks, 'row', axis=0, tiled=True, axis_index_groups=pairs)  4.47 us
    pallas_call x1, Pallas kernels, multiplied(): pl.pallas_call(lambda *refs: multiplying(zs, *refs), in_specs=[pl.BlockSp...  3.08 us
    pallas_call x1, Pallas kernels, contracted(): pl.pallas_call(lambda *refs: contracting(zs, *refs), out_shape=[jax.Shape...  1.5 us

profile of v4, /device:TPU:1, one launch (start us, length us, event | category | flops | bytes accessed | tf_op | source)
XLA Modules:
  0.0 71.3 jit_solution(9691318014123006586)
XLA Ops:
  0.6 0.0 copy-start
  0.6 3.1 %multiplying.1 = (f32[64,640]{1,0:T(8,128)S(1)}, f32[64,640]{1,0:T(8,128)S(1)}, f32[64,128]{1,0:T(8,128)S(1)}) custom-call(bf16[64,2048]{1,0:T(8,128)(2,1)} %refs_0_.1, bf16[2048,1024]{1,0:T(8,128)(2,1)} %refs_1_.3, f32[64,1024]{1,0:T(8,128)} %refs_2_.1), custom_call_target="tpu_custom_call" | custom-call | tf_op jit(solution)/shard_map/multiplying/pallas_call | solution.py:86
  3.7 8.5 %all_gather.6.refs_1_ = f32[128,640]{1,0:T(8,128)S(1)} all-gather(f32[64,640]{1,0:T(8,128)S(1)} %get-tuple-element.9), channel_id=1, replica_groups={{0,32},{64,96},{128,160},{192,224},{256,288},{320,352},{384,416},{448,4..., dimensions={0}, use_global_device_ids=true | all-gather | bytes 491520 | tf_op jit(solution)/shard_map/all_gather | solution.py:300
  12.2 0.1 packing.1
  12.3 15.6 %all_to_all.32 = f32[8,64,128]{2,1,0:T(8,128)S(1)} all-to-all(f32[8,64,128]{2,1,0:T(8,128)S(1)} %bitcast.8), channel_id=1, replica_groups={{0,64,128,192,256,320,384,448},{32,96,160,224,288,352,416,480},{1,65,12..., dimensions={0} | all-to-all | bytes 524288 | tf_op jit(solution)/shard_map/all_to_all | solution.py:302
  28.0 0.8 %iterating.1 = f32[256,128]{1,0:T(8,128)S(1)} custom-call(f32[512,128]{1,0:T(8,128)S(1)} %bitcast.9, f32[64,128]{1,0:T(8,128)S(1)} %get-tuple-element.10.refs_1_), custom_call_target="tpu_custom_call" | custom-call | tf_op jit(solution)/shard_map/iterating/pallas_call | solution.py:153
  28.8 10.3 %all_to_all.33 = f32[8,32,128]{2,1,0:T(8,128)S(1)} all-to-all(f32[8,32,128]{2,1,0:T(8,128)S(1)} %bitcast.10), channel_id=1, replica_groups={{0,64,128,192,256,320,384,448},{32,96,160,224,288,352,416,480},{1,65,12..., dimensions={0} | all-to-all | bytes 262144 | tf_op jit(solution)/shard_map/all_to_all | solution.py:304
  39.1 4.5 %all_gather.7.refs_0_ = f32[512,128]{1,0:T(8,128)S(1)} all-gather(f32[256,128]{1,0:T(8,128)S(1)} %bitcast.12), channel_id=1, replica_groups={{0,32},{64,96},{128,160},{192,224},{256,288},{320,352},{384,416},{448,4..., dimensions={0}, use_global_device_ids=true | all-gather | bytes 393216 | tf_op jit(solution)/shard_map/all_gather | solution.py:305
  43.6 0.0 copy-done
  43.6 1.5 %contracting.1 = (f32[64,1024]{1,0:T(8,128)S(1)}, f32[1792,128]{1,0:T(8,128)S(1)}) custom-call(f32[512,128]{1,0:T(8,128)S(1)} %all_gather.7.refs_0_, bf16[2048,1024]{1,0:T(8,128)(2,1)S(1)} %copy-done), custom_call_target="tpu_custom_call" | custom-call | tf_op jit(solution)/shard_map/contracting/pallas_call | solution.py:227
  45.1 0.1 convert_element_type.8
  45.2 25.0 %all_to_all.34 = f16[32,56,128]{2,1,0:T(8,128)(2,1)S(1)} all-to-all(f16[32,56,128]{2,1,0:T(8,128)(2,1)S(1)} %bitcast.11), channel_id=1, replica_groups=mesh['row'=16,'col'=32] {'col'}, dimensions={0} | all-to-all | bytes 917504 | tf_op jit(solution)/shard_map/all_to_all | solution.py:307
  70.2 0.1 bitcast_convert_fusion.refs_0_
  70.3 1.1 %finishing.1 = (bf16[64,1024]{1,0:T(8,128)(2,1)}, f32[64,64]{1,0:T(8,128)}, f32[64,64]{1,0:T(8,128)}) custom-call(f32[1792,128]{1,0:T(8,128)S(1)} %bitcast_convert_fusion.refs_0_, f32[64,1024]{1,0:T(8,128)S(1)} %get-tuple-element.12.refs_1_), custom_call_target="tpu_custom_call" | custom-call | tf_op jit(solution)/shard_map/finishing/pallas_call | solution.py:279
Async XLA Ops:
  0.6 43.0 %copy-start = (bf16[2048,1024]{1,0:T(8,128)(2,1)S(1)}, bf16[2048,1024]{1,0:T(8,128)(2,1)}, u32[]{:S(2)}) copy-start(bf16[2048,1024]{1,0:T(8,128)(2,1)} %refs_1_.3) | copy-start | bytes 12582916

commit v5 on v4

--- a/solution.py
+++ b/solution.py
@@ -12,6 +12,8 @@
 LANES = 128
 HALF = 64
 BLOCKS = 4
+STOPS = (6, 11, 14, 16)
+PART = 56
 CHUNK = 56
 MIB = 1 << 20
 
@@ -39,18 +41,19 @@
 def multiplying(zs, w_hbm, data_hbm, h_hbm, own_ref, send_ref, start_ref, data_ref, w, h, acc, sems):
     rows, columns = data_ref.shape
     width = columns // 2
-    depth = rows // BLOCKS
+    ends = [rows * part // 16 for part in STOPS]
+    spans = list(zip([0, *ends], ends))
     me = lax.axis_index("row")
     core, level = lax.rem(me, 2), lax.div(me, 2)
     tile = core * (width // LANES) + lax.div(level, 2)
     copies = [
-        pltpu.make_async_copy(w_hbm, w, sems.at[BLOCKS]),
+        pltpu.make_async_copy(w_hbm, w, sems.at[len(STOPS)]),
         pltpu.make_async_copy(
-            h_hbm.at[:, pl.ds(pl.multiple_of(tile * LANES, LANES), LANES)], h, sems.at[BLOCKS + 1]
+            h_hbm.at[:, pl.ds(pl.multiple_of(tile * LANES, LANES), LANES)], h, sems.at[len(STOPS) + 1]
         ),
     ]
-    for block in range(BLOCKS):
-        at = pl.ds(block * depth, depth)
+    for block, (begin, end) in enumerate(spans):
+        at = pl.ds(begin, end - begin)
         copies.append(pltpu.make_async_copy(data_hbm.at[at, :], data_ref.at[at, :], sems.at[block]))
     for copy in (copies[0], *copies[2:], copies[1]):
         copy.start()
@@ -60,9 +63,9 @@
     )
     own_ref[:, width:] = gram
     send_ref[:, width:] = gram
-    for block in range(BLOCKS):
+    for block, (begin, end) in enumerate(spans):
         copies[2 + block].wait()
-        at = slice(block * depth, (block + 1) * depth)
+        at = slice(begin, end)
         part = jnp.dot(w[:, at], data_ref[at, :], preferred_element_type=jnp.float32)
         if block == 0:
             acc[...] = part
@@ -93,44 +96,69 @@
             pltpu.VMEM(w_rows.shape, w_rows.dtype),
             pltpu.VMEM((rank, LANES), jnp.float32),
             pltpu.VMEM((rank, columns), jnp.float32),
-            pltpu.SemaphoreType.DMA((BLOCKS + 2,)),
+            pltpu.SemaphoreType.DMA((len(STOPS) + 2,)),
         ],
         compiler_params=pltpu.CompilerParams(vmem_limit_bytes=56045568),
         name="multiplying",
     )(w_rows, data, h_init)
 
 
+def folded_of(outer):
+    top, low = outer[:32], outer[32:]
+    lane = lax.broadcasted_iota(jnp.int32, top.shape, 1)
+    row = lax.broadcasted_iota(jnp.int32, top.shape, 0)
+    folded = jnp.where((lane % HALF < 32) & (row > lane % 32), pltpu.roll(low, 96, 1), top)
+    return jnp.where(low_lanes(folded[:16]), folded[:16], folded[16:])
+
+
+def unfolded(folded, diagonal):
+    upper = jnp.concatenate([folded, turned(folded)], axis=0)
+    upper = jnp.concatenate([upper, pltpu.roll(upper, 32, 1)], axis=0)
+    mirror = jnp.transpose(upper)[:HALF, :]
+    upper = upper[:, :HALF]
+    row = lax.broadcasted_iota(jnp.int32, upper.shape, 0)
+    lane = lax.broadcasted_iota(jnp.int32, upper.shape, 1)
+    held = ((row < 32) & (row < lane)) | ((lane >= 32) & (row > lane))
+    return jnp.where(row == lane, diagonal, jnp.where(held, upper, mirror))
+
+
 def packing(zs, own_ref, got_ref, out_ref):
     width = own_ref.shape[1] - LANES
     rank = own_ref.shape[0]
     theirs = pl.ds(pl.multiple_of((1 - lax.rem(lax.axis_index("row"), 2)) * rank, 8), rank)
-    gram = stack_copies(own_ref[:, width:] + got_ref[theirs, width:])
+    whole = own_ref[:, width:] + got_ref[theirs, width:]
+    gram = folded_of(whole)
+    row = lax.broadcasted_iota(jnp.int32, whole.shape, 0)
+    lane = lax.broadcasted_iota(jnp.int32, whole.shape, 1)
+    diagonal = jnp.sum(jnp.where(row == lane % HALF, whole, 0.0), axis=0, keepdims=True)
+    diagonal = jnp.broadcast_to(diagonal, (8, LANES))
     for tile in range(width // LANES):
         at = slice(tile * LANES, (tile + 1) * LANES)
         x = own_ref[:, at] + got_ref[theirs, at]
         top, low = x[:32], x[32:]
         left = low_lanes(top)
         for side, block in enumerate((jnp.where(left, top, turned(low)), jnp.where(left, turned(top), low))):
-            base = (2 * tile + side) * 64
+            base = (2 * tile + side) * PART
             out_ref[base : base + 32, :] = block
-            out_ref[base + 32 : base + 64, :] = gram
+            out_ref[base + 32 : base + 48, :] = gram
+            out_ref[base + 48 : base + 56, :] = diagonal
 
 
 def packed(zs, own, got):
     return pl.pallas_call(
         lambda *refs: packing(zs, *refs),
-        out_shape=jax.ShapeDtypeStruct((zs * 64, LANES), jnp.float32),
+        out_shape=jax.ShapeDtypeStruct((zs * PART, LANES), jnp.float32),
         compiler_params=pltpu.CompilerParams(vmem_limit_bytes=8 * MIB),
         name="packing",
     )(own, got)
 
 
 def iterating(zs, got_ref, start_ref, out_ref):
-    total = got_ref[0:64, :]
+    total = got_ref[0:PART, :]
     for part in range(1, zs):
-        total = total + got_ref[part * 64 : part * 64 + 64, :]
+        total = total + got_ref[part * PART : part * PART + PART, :]
+    gram = unfolded(total[32:48], total[48:49, :HALF])
     target = unstack(total[:32])
-    gram = unstack(total[32:])[:, :HALF]
     lip = jnp.max(jnp.sum(gram, axis=1, keepdims=True))
     factor = start_ref[...]
     ahead = factor
@@ -203,11 +231,7 @@
         jnp.where(line == 1, power, jnp.where(line == 2, power + most, 0.0)),
     )
     outer = outer * (shrink * jnp.exp2(-most) * 32768.0)
-    top, low = outer[:32], outer[32:]
-    lane = lax.broadcasted_iota(jnp.int32, top.shape, 1)
-    row = lax.broadcasted_iota(jnp.int32, top.shape, 0)
-    folded = jnp.where((lane % HALF < 32) & (row > lane % 32), pltpu.roll(low, 96, 1), top)
-    folded = jnp.where(low_lanes(folded[:16]), folded[:16], folded[16:])
+    folded = folded_of(outer)
     shrink = shrink * 1024.0
 
     parts = data_ref.shape[0] // 64
@@ -253,14 +277,9 @@
         folded = folded + got_ref[base + 32 : base + 48, :] * jnp.where(swapped, pltpu.roll(pair, 96, 1), pair)
         squares = squares + (extra[0:1, :] + turned(extra[0:1, :])) * (grow * grow)
     squares = squares[:, :HALF] * (1.0 / 32768.0)
-    upper = jnp.concatenate([folded, turned(folded)], axis=0) * (1.0 / 32768.0)
-    upper = jnp.concatenate([upper, pltpu.roll(upper, 32, 1)], axis=0)
-    mirror = jnp.transpose(upper)[:HALF, :]
-    upper = upper[:, :HALF]
-    row = lax.broadcasted_iota(jnp.int32, upper.shape, 0)
-    lane = lax.broadcasted_iota(jnp.int32, upper.shape, 1)
-    held = ((row < 32) & (row < lane)) | ((lane >= 32) & (row > lane))
-    outer = jnp.where(row == lane, squares, jnp.where(held, upper, mirror))
+    outer = unfolded(folded * (1.0 / 32768.0), squares)
+    row = lax.broadcasted_iota(jnp.int32, outer.shape, 0)
+    lane = lax.broadcasted_iota(jnp.int32, outer.shape, 1)
 
     def scale_of(squares):
         mean = squares / columns + 1e-06

time: 71.6 us -> 70.8 us (0.989)
    all_to_all x1, blocking collectives: 15.6 us -> 14.7 us  [shards(): lax.all_to_all(parts, 'row', 0, 0, tiled=True, axis_index_groups=levels)]
where the time goes in v5:
time: 70.8 us; the launch traced here: 70.5 us
  blocking collectives  63.2 us (89%)
  Pallas kernels  6.48 us (9%)
    all_to_all x1, blocking collectives, shards(): sums = lax.all_to_all(terms.astype(jnp.float16), 'col', 0, 0, tiled=True)  25 us
    all_to_all x1, blocking collectives, shards(): lax.all_to_all(parts, 'row', 0, 0, tiled=True, axis_index_groups=levels)  14.7 us
    all_to_all x1, blocking collectives, shards(): lax.all_to_all(copies, 'row', 0, 0, tiled=True, axis_index_groups=levels)  10.4 us
    all_gather x1, blocking collectives, shards(): lax.all_gather(send, 'row', axis=0, tiled=True, axis_index_groups=pairs)  8.51 us
    all_gather x1, blocking collectives, shards(): lax.all_gather(blocks, 'row', axis=0, tiled=True, axis_index_groups=pairs)  4.63 us
    pallas_call x1, Pallas kernels, multiplied(): pl.pallas_call(lambda *refs: multiplying(zs, *refs), in_specs=[pl.BlockSp...  2.85 us
    pallas_call x1, Pallas kernels, contracted(): pl.pallas_call(lambda *refs: contracting(zs, *refs), out_shape=[jax.Shape...  1.5 us

profile of v5, /device:TPU:1, one launch (start us, length us, event | category | flops | bytes accessed | tf_op | source)
XLA Modules:
  0.0 70.5 jit_solution(16370521430108814439)
XLA Ops:
  0.6 0.0 copy-start
  0.6 2.9 %multiplying.1 = (f32[64,640]{1,0:T(8,128)S(1)}, f32[64,640]{1,0:T(8,128)S(1)}, f32[64,128]{1,0:T(8,128)S(1)}) custom-call(bf16[64,2048]{1,0:T(8,128)(2,1)} %refs_0_.1, bf16[2048,1024]{1,0:T(8,128)(2,1)} %refs_1_.3, f32[64,1024]{1,0:T(8,128)} %refs_2_.1), custom_call_target="tpu_custom_call" | custom-call | tf_op jit(solution)/shard_map/multiplying/pallas_call | solution.py:89
  3.5 8.5 %all_gather.6.refs_1_ = f32[128,640]{1,0:T(8,128)S(1)} all-gather(f32[64,640]{1,0:T(8,128)S(1)} %get-tuple-element.9), channel_id=1, replica_groups={{0,32},{64,96},{128,160},{192,224},{256,288},{320,352},{384,416},{448,4..., dimensions={0}, use_global_device_ids=true | all-gather | bytes 491520 | tf_op jit(solution)/shard_map/all_gather | solution.py:319
  12.0 0.1 packing.1
  12.1 14.7 %all_to_all.32 = f32[8,56,128]{2,1,0:T(8,128)S(1)} all-to-all(f32[8,56,128]{2,1,0:T(8,128)S(1)} %bitcast.9), channel_id=1, replica_groups={{0,64,128,192,256,320,384,448},{32,96,160,224,288,352,416,480},{1,65,12..., dimensions={0} | all-to-all | bytes 458752 | tf_op jit(solution)/shard_map/all_to_all | solution.py:321
  26.8 1.0 %iterating.1 = f32[256,128]{1,0:T(8,128)S(1)} custom-call(f32[448,128]{1,0:T(8,128)S(1)} %bitcast.8, f32[64,128]{1,0:T(8,128)S(1)} %get-tuple-element.10.refs_1_), custom_call_target="tpu_custom_call" | custom-call | tf_op jit(solution)/shard_map/iterating/pallas_call | solution.py:181
  27.8 10.4 %all_to_all.33 = f32[8,32,128]{2,1,0:T(8,128)S(1)} all-to-all(f32[8,32,128]{2,1,0:T(8,128)S(1)} %bitcast.10), channel_id=1, replica_groups={{0,64,128,192,256,320,384,448},{32,96,160,224,288,352,416,480},{1,65,12..., dimensions={0} | all-to-all | bytes 262144 | tf_op jit(solution)/shard_map/all_to_all | solution.py:323
  38.2 4.6 %all_gather.7.refs_0_ = f32[512,128]{1,0:T(8,128)S(1)} all-gather(f32[256,128]{1,0:T(8,128)S(1)} %bitcast.12), channel_id=1, replica_groups={{0,32},{64,96},{128,160},{192,224},{256,288},{320,352},{384,416},{448,4..., dimensions={0}, use_global_device_ids=true | all-gather | bytes 393216 | tf_op jit(solution)/shard_map/all_gather | solution.py:324
  42.8 0.0 copy-done
  42.8 1.5 %contracting.1 = (f32[64,1024]{1,0:T(8,128)S(1)}, f32[1792,128]{1,0:T(8,128)S(1)}) custom-call(f32[512,128]{1,0:T(8,128)S(1)} %all_gather.7.refs_0_, bf16[2048,1024]{1,0:T(8,128)(2,1)S(1)} %copy-done), custom_call_target="tpu_custom_call" | custom-call | tf_op jit(solution)/shard_map/contracting/pallas_call | solution.py:251
  44.3 0.1 convert_element_type.8
  44.4 25.0 %all_to_all.34 = f16[32,56,128]{2,1,0:T(8,128)(2,1)S(1)} all-to-all(f16[32,56,128]{2,1,0:T(8,128)(2,1)S(1)} %bitcast.11), channel_id=1, replica_groups=mesh['row'=16,'col'=32] {'col'}, dimensions={0} | all-to-all | bytes 917504 | tf_op jit(solution)/shard_map/all_to_all | solution.py:326
  69.4 0.1 bitcast_convert_fusion.refs_0_
  69.5 1.0 %finishing.1 = (bf16[64,1024]{1,0:T(8,128)(2,1)}, f32[64,64]{1,0:T(8,128)}, f32[64,64]{1,0:T(8,128)}) custom-call(f32[1792,128]{1,0:T(8,128)S(1)} %bitcast_convert_fusion.refs_0_, f32[64,1024]{1,0:T(8,128)S(1)} %get-tuple-element.12.refs_1_), custom_call_target="tpu_custom_call" | custom-call | tf_op jit(solution)/shard_map/finishing/pallas_call | solution.py:298
Async XLA Ops:
  0.6 42.2 %copy-start = (bf16[2048,1024]{1,0:T(8,128)(2,1)S(1)}, bf16[2048,1024]{1,0:T(8,128)(2,1)}, u32[]{:S(2)}) copy-start(bf16[2048,1024]{1,0:T(8,128)(2,1)} %refs_1_.3) | copy-start | bytes 12582916

commit v6 on v5

--- a/solution.py
+++ b/solution.py
@@ -215,7 +215,7 @@
     ones = jnp.ones((8, lines.shape[1]), jnp.bfloat16)
     sums = lax.dot_general(ones, lines[...], both, preferred_element_type=jnp.float32)[0:1, :]
     power = jnp.ceil(jnp.log(jnp.maximum(sums, 1e-30)) * LOG2E)
-    power = jnp.clip(power, -60.0, 60.0)
+    power = jnp.clip(power, -40.0, 60.0)
     most = jnp.max(power, axis=1, keepdims=True)
     shrink = jnp.exp2(-power)
     row = lax.broadcasted_iota(jnp.int32, outer.shape, 0)
@@ -230,7 +230,7 @@
         jnp.where(low_lanes(high), high, across - high),
         jnp.where(line == 1, power, jnp.where(line == 2, power + most, 0.0)),
     )
-    outer = outer * (shrink * jnp.exp2(-most) * 32768.0)
+    outer = (outer * shrink) * (jnp.exp2(-most) * 32768.0)
     folded = folded_of(outer)
     shrink = shrink * 1024.0
 

time: 70.8 us -> 70.8 us (level)
  no operation moved by 1% of the time
where the time goes in v6:
time: 70.8 us; the launch traced here: 70.5 us
  blocking collectives  63.2 us (89%)
  Pallas kernels  6.48 us (9%)
    all_to_all x1, blocking collectives, shards(): sums = lax.all_to_all(terms.astype(jnp.float16), 'col', 0, 0, tiled=True)  25 us
    all_to_all x1, blocking collectives, shards(): lax.all_to_all(parts, 'row', 0, 0, tiled=True, axis_index_groups=levels)  14.7 us
    all_to_all x1, blocking collectives, shards(): lax.all_to_all(copies, 'row', 0, 0, tiled=True, axis_index_groups=levels)  10.4 us
    all_gather x1, blocking collectives, shards(): lax.all_gather(send, 'row', axis=0, tiled=True, axis_index_groups=pairs)  8.51 us
    all_gather x1, blocking collectives, shards(): lax.all_gather(blocks, 'row', axis=0, tiled=True, axis_index_groups=pairs)  4.63 us
    pallas_call x1, Pallas kernels, multiplied(): pl.pallas_call(lambda *refs: multiplying(zs, *refs), in_specs=[pl.BlockSp...  2.85 us
    pallas_call x1, Pallas kernels, contracted(): pl.pallas_call(lambda *refs: contracting(zs, *refs), out_shape=[jax.Shape...  1.5 us

profile of v6, /device:TPU:1, one launch (start us, length us, event | category | flops | bytes accessed | tf_op | source)
XLA Modules:
  0.0 70.5 jit_solution(16166646575657107980)
XLA Ops:
  0.6 0.0 copy-start
  0.6 2.9 %multiplying.1 = (f32[64,640]{1,0:T(8,128)S(1)}, f32[64,640]{1,0:T(8,128)S(1)}, f32[64,128]{1,0:T(8,128)S(1)}) custom-call(bf16[64,2048]{1,0:T(8,128)(2,1)} %refs_0_.1, bf16[2048,1024]{1,0:T(8,128)(2,1)} %refs_1_.3, f32[64,1024]{1,0:T(8,128)} %refs_2_.1), custom_call_target="tpu_custom_call" | custom-call | tf_op jit(solution)/shard_map/multiplying/pallas_call | solution.py:89
  3.5 8.5 %all_gather.6.refs_1_ = f32[128,640]{1,0:T(8,128)S(1)} all-gather(f32[64,640]{1,0:T(8,128)S(1)} %get-tuple-element.9), channel_id=1, replica_groups={{0,32},{64,96},{128,160},{192,224},{256,288},{320,352},{384,416},{448,4..., dimensions={0}, use_global_device_ids=true | all-gather | bytes 491520 | tf_op jit(solution)/shard_map/all_gather | solution.py:319
  12.0 0.1 packing.1
  12.1 14.7 %all_to_all.32 = f32[8,56,128]{2,1,0:T(8,128)S(1)} all-to-all(f32[8,56,128]{2,1,0:T(8,128)S(1)} %bitcast.9), channel_id=1, replica_groups={{0,64,128,192,256,320,384,448},{32,96,160,224,288,352,416,480},{1,65,12..., dimensions={0} | all-to-all | bytes 458752 | tf_op jit(solution)/shard_map/all_to_all | solution.py:321
  26.8 1.0 %iterating.1 = f32[256,128]{1,0:T(8,128)S(1)} custom-call(f32[448,128]{1,0:T(8,128)S(1)} %bitcast.8, f32[64,128]{1,0:T(8,128)S(1)} %get-tuple-element.10.refs_1_), custom_call_target="tpu_custom_call" | custom-call | tf_op jit(solution)/shard_map/iterating/pallas_call | solution.py:181
  27.8 10.4 %all_to_all.33 = f32[8,32,128]{2,1,0:T(8,128)S(1)} all-to-all(f32[8,32,128]{2,1,0:T(8,128)S(1)} %bitcast.10), channel_id=1, replica_groups={{0,64,128,192,256,320,384,448},{32,96,160,224,288,352,416,480},{1,65,12..., dimensions={0} | all-to-all | bytes 262144 | tf_op jit(solution)/shard_map/all_to_all | solution.py:323
  38.2 4.6 %all_gather.7.refs_0_ = f32[512,128]{1,0:T(8,128)S(1)} all-gather(f32[256,128]{1,0:T(8,128)S(1)} %bitcast.12), channel_id=1, replica_groups={{0,32},{64,96},{128,160},{192,224},{256,288},{320,352},{384,416},{448,4..., dimensions={0}, use_global_device_ids=true | all-gather | bytes 393216 | tf_op jit(solution)/shard_map/all_gather | solution.py:324
  42.8 0.0 copy-done
  42.8 1.5 %contracting.1 = (f32[64,1024]{1,0:T(8,128)S(1)}, f32[1792,128]{1,0:T(8,128)S(1)}) custom-call(f32[512,128]{1,0:T(8,128)S(1)} %all_gather.7.refs_0_, bf16[2048,1024]{1,0:T(8,128)(2,1)S(1)} %copy-done), custom_call_target="tpu_custom_call" | custom-call | tf_op jit(solution)/shard_map/contracting/pallas_call | solution.py:251
  44.3 0.1 convert_element_type.8
  44.4 25.0 %all_to_all.34 = f16[32,56,128]{2,1,0:T(8,128)(2,1)S(1)} all-to-all(f16[32,56,128]{2,1,0:T(8,128)(2,1)S(1)} %bitcast.11), channel_id=1, replica_groups=mesh['row'=16,'col'=32] {'col'}, dimensions={0} | all-to-all | bytes 917504 | tf_op jit(solution)/shard_map/all_to_all | solution.py:326
  69.4 0.1 bitcast_convert_fusion.refs_0_
  69.5 1.0 %finishing.1 = (bf16[64,1024]{1,0:T(8,128)(2,1)}, f32[64,64]{1,0:T(8,128)}, f32[64,64]{1,0:T(8,128)}) custom-call(f32[1792,128]{1,0:T(8,128)S(1)} %bitcast_convert_fusion.refs_0_, f32[64,1024]{1,0:T(8,128)S(1)} %get-tuple-element.12.refs_1_), custom_call_target="tpu_custom_call" | custom-call | tf_op jit(solution)/shard_map/finishing/pallas_call | solution.py:298
Async XLA Ops:
  0.6 42.2 %copy-start = (bf16[2048,1024]{1,0:T(8,128)(2,1)S(1)}, bf16[2048,1024]{1,0:T(8,128)(2,1)}, u32[]{:S(2)}) copy-start(bf16[2048,1024]{1,0:T(8,128)(2,1)} %refs_1_.3) | copy-start | bytes 12582916

commit v7 on v6

--- a/solution.py
+++ b/solution.py
@@ -153,21 +153,31 @@
     )(own, got)
 
 
+def split(x):
+    one = x.astype(jnp.bfloat16)
+    rest = x - one.astype(jnp.float32)
+    two = rest.astype(jnp.bfloat16)
+    three = (rest - two.astype(jnp.float32)).astype(jnp.bfloat16)
+    return one, two, three
+
+
 def iterating(zs, got_ref, start_ref, out_ref):
     total = got_ref[0:PART, :]
     for part in range(1, zs):
         total = total + got_ref[part * PART : part * PART + PART, :]
     gram = unfolded(total[32:48], total[48:49, :HALF])
     target = unstack(total[:32])
-    lip = jnp.max(jnp.sum(gram, axis=1, keepdims=True))
+    inverse = 1.0 / jnp.max(jnp.sum(gram, axis=0, keepdims=True))
+    one, two, three = split(gram)
+    left = jnp.concatenate([one, one, two, one, two, three], axis=1)
     factor = start_ref[...]
     ahead = factor
     momentum = 1.0
     for step in range(ITERS):
-        slope = jnp.dot(
-            gram, ahead, precision=lax.Precision.HIGHEST, preferred_element_type=jnp.float32
-        ) - target
-        fresh = jnp.maximum(ahead - slope / lip, 0.0)
+        one, two, three = split(ahead)
+        right = jnp.concatenate([one, two, one, three, two, one], axis=0)
+        slope = jnp.dot(left, right, preferred_element_type=jnp.float32) - target
+        fresh = jnp.maximum(ahead - slope * inverse, 0.0)
         following = (1.0 + math.sqrt(1.0 + 4.0 * momentum * momentum)) / 2.0
         ahead = fresh + (momentum - 1.0) / following * (fresh - factor)
         factor = fresh

time: 70.8 us -> 70.7 us (level)
  no operation moved by 1% of the time
where the time goes in v7:
time: 70.7 us; the launch traced here: 70.5 us
  blocking collectives  63.2 us (89%)
  Pallas kernels  6.44 us (9%)
    all_to_all x1, blocking collectives, shards(): sums = lax.all_to_all(terms.astype(jnp.float16), 'col', 0, 0, tiled=True)  25 us
    all_to_all x1, blocking collectives, shards(): lax.all_to_all(parts, 'row', 0, 0, tiled=True, axis_index_groups=levels)  14.7 us
    all_to_all x1, blocking collectives, shards(): lax.all_to_all(copies, 'row', 0, 0, tiled=True, axis_index_groups=levels)  10.4 us
    all_gather x1, blocking collectives, shards(): lax.all_gather(send, 'row', axis=0, tiled=True, axis_index_groups=pairs)  8.51 us
    all_gather x1, blocking collectives, shards(): lax.all_gather(blocks, 'row', axis=0, tiled=True, axis_index_groups=pairs)  4.63 us
    pallas_call x1, Pallas kernels, multiplied(): pl.pallas_call(lambda *refs: multiplying(zs, *refs), in_specs=[pl.BlockSp...  2.85 us
    pallas_call x1, Pallas kernels, contracted(): pl.pallas_call(lambda *refs: contracting(zs, *refs), out_shape=[jax.Shape...  1.5 us

profile of v7, /device:TPU:1, one launch (start us, length us, event | category | flops | bytes accessed | tf_op | source)
XLA Modules:
  0.0 70.5 jit_solution(3721305419466315416)
XLA Ops:
  0.6 0.0 copy-start
  0.6 2.9 %multiplying.1 = (f32[64,640]{1,0:T(8,128)S(1)}, f32[64,640]{1,0:T(8,128)S(1)}, f32[64,128]{1,0:T(8,128)S(1)}) custom-call(bf16[64,2048]{1,0:T(8,128)(2,1)} %refs_0_.1, bf16[2048,1024]{1,0:T(8,128)(2,1)} %refs_1_.3, f32[64,1024]{1,0:T(8,128)} %refs_2_.1), custom_call_target="tpu_custom_call" | custom-call | tf_op jit(solution)/shard_map/multiplying/pallas_call | solution.py:89
  3.5 8.5 %all_gather.6.refs_1_ = f32[128,640]{1,0:T(8,128)S(1)} all-gather(f32[64,640]{1,0:T(8,128)S(1)} %get-tuple-element.9), channel_id=1, replica_groups={{0,32},{64,96},{128,160},{192,224},{256,288},{320,352},{384,416},{448,4..., dimensions={0}, use_global_device_ids=true | all-gather | bytes 491520 | tf_op jit(solution)/shard_map/all_gather | solution.py:329
  12.0 0.1 packing.1
  12.1 14.7 %all_to_all.32 = f32[8,56,128]{2,1,0:T(8,128)S(1)} all-to-all(f32[8,56,128]{2,1,0:T(8,128)S(1)} %bitcast.9), channel_id=1, replica_groups={{0,64,128,192,256,320,384,448},{32,96,160,224,288,352,416,480},{1,65,12..., dimensions={0} | all-to-all | bytes 458752 | tf_op jit(solution)/shard_map/all_to_all | solution.py:331
  26.8 0.9 %iterating.1 = f32[256,128]{1,0:T(8,128)S(1)} custom-call(f32[448,128]{1,0:T(8,128)S(1)} %bitcast.8, f32[64,128]{1,0:T(8,128)S(1)} %get-tuple-element.10.refs_1_), custom_call_target="tpu_custom_call" | custom-call | tf_op jit(solution)/shard_map/iterating/pallas_call | solution.py:191
  27.7 10.4 %all_to_all.33 = f32[8,32,128]{2,1,0:T(8,128)S(1)} all-to-all(f32[8,32,128]{2,1,0:T(8,128)S(1)} %bitcast.10), channel_id=1, replica_groups={{0,64,128,192,256,320,384,448},{32,96,160,224,288,352,416,480},{1,65,12..., dimensions={0} | all-to-all | bytes 262144 | tf_op jit(solution)/shard_map/all_to_all | solution.py:333
  38.1 4.6 %all_gather.7.refs_0_ = f32[512,128]{1,0:T(8,128)S(1)} all-gather(f32[256,128]{1,0:T(8,128)S(1)} %bitcast.12), channel_id=1, replica_groups={{0,32},{64,96},{128,160},{192,224},{256,288},{320,352},{384,416},{448,4..., dimensions={0}, use_global_device_ids=true | all-gather | bytes 393216 | tf_op jit(solution)/shard_map/all_gather | solution.py:334
  42.8 0.0 copy-done
  42.8 1.5 %contracting.1 = (f32[64,1024]{1,0:T(8,128)S(1)}, f32[1792,128]{1,0:T(8,128)S(1)}) custom-call(f32[512,128]{1,0:T(8,128)S(1)} %all_gather.7.refs_0_, bf16[2048,1024]{1,0:T(8,128)(2,1)S(1)} %copy-done), custom_call_target="tpu_custom_call" | custom-call | tf_op jit(solution)/shard_map/contracting/pallas_call | solution.py:261
  44.3 0.1 convert_element_type.8
  44.3 25.0 %all_to_all.34 = f16[32,56,128]{2,1,0:T(8,128)(2,1)S(1)} all-to-all(f16[32,56,128]{2,1,0:T(8,128)(2,1)S(1)} %bitcast.11), channel_id=1, replica_groups=mesh['row'=16,'col'=32] {'col'}, dimensions={0} | all-to-all | bytes 917504 | tf_op jit(solution)/shard_map/all_to_all | solution.py:336
  69.3 0.1 bitcast_convert_fusion.refs_0_
  69.4 1.0 %finishing.1 = (bf16[64,1024]{1,0:T(8,128)(2,1)}, f32[64,64]{1,0:T(8,128)}, f32[64,64]{1,0:T(8,128)}) custom-call(f32[1792,128]{1,0:T(8,128)S(1)} %bitcast_convert_fusion.refs_0_, f32[64,1024]{1,0:T(8,128)S(1)} %get-tuple-element.12.refs_1_), custom_call_target="tpu_custom_call" | custom-call | tf_op jit(solution)/shard_map/finishing/pallas_call | solution.py:308
Async XLA Ops:
  0.6 42.1 %copy-start = (bf16[2048,1024]{1,0:T(8,128)(2,1)S(1)}, bf16[2048,1024]{1,0:T(8,128)(2,1)}, u32[]{:S(2)}) copy-start(bf16[2048,1024]{1,0:T(8,128)(2,1)} %refs_1_.3) | copy-start | bytes 12582916
